TPU v7x, 128 devices: a whole 4x4x4 slice. The times are simulated.
128 devices in a mesh: dp: 4 (over z_hi, core), seq: 32 (over y, x, z_lo).
Axes of the slice: x: 4, y: 4, z: 4 (z_hi: 2, z_lo: 2; z = z_hi * 2 + z_lo), core: 2. Of those that a mesh axis runs over, the one named last changes fastest.
Arguments:
- tile_embed: bfloat16 [4, 4096, 768], P('dp', 'seq'), may hold values from -6 to 6
- qkv_saved: bfloat16 [4, 4096, 1152], P('dp', 'seq'), may hold values from -8 to 8
- out_cotangent: bfloat16 [4, 4096, 768], P('dp', 'seq'), may hold values from -6 to 6
- qkv_weight: bfloat16 [768, 1152], replicated, may hold values from -0.21875 to 0.21875
- out_weight: bfloat16 [384, 768], replicated, may hold values from -0.3125 to 0.3125
- seg_length: int32 [8], replicated, may hold values from 128 to 4096, as said below
- dilation: int32 [8], replicated, may hold values from 1 to 4
- owner_map: int32 [4, 4096, 1], P('dp', 'seq'), may hold values from 0 to 31; in each aligned block of 128 rows (0 to 127, 128 to 255, ..., all dimensions but the last counted through in order) at most 8 rows name the same one
- tile_hidden: bfloat16 [4, 8192, 1536], P('dp', 'seq'), may hold values from -6 to 6
- tile_output: bfloat16 [4, 8192, 1536], P('dp', 'seq'), may hold values from -6 to 6
- embed_weight: bfloat16 [1536, 768], replicated, may hold values from -0.15625 to 0.15625
- proj_weight: bfloat16 [1536, 1536], replicated, may hold values from -0.15625 to 0.15625
Outputs:
- hidden_grad: bfloat16 [4, 8192, 1536], P('dp', 'seq')
- proj_weight_grad: float32 [1536, 1536], P(('dp', 'seq'))
- embed_weight_grad: float32 [1536, 768], P(('dp', 'seq'))
- qkv_weight_grad: float32 [768, 1152], P(('dp', 'seq'))
- out_weight_grad: float32 [384, 768], P(('dp', 'seq'))
Inputs may be any that keep to these rules, and one draw needn't show every extreme that they name: `seg_length`: each is 128 times a power of two; some head has 4096. `owner_map`: among the 128 positions of one device, no device index is named more than 8 times.
All inputs are finite; a program needn't handle non-finite values.
Results may differ from a plain program's by a relative error of at most 0.015.
Values may be sent and summed in bfloat16 or wider, within the bound.
No kernel may reach another device: no remote copies, remote signals or barrier semaphores. Data moves between devices by JAX's collectives and lax.ppermute only.
A program may use at most 128 MiB of HBM per device.

v0:
```python
from functools import partial

import jax
import jax.numpy as jnp
from jax import lax
from jax.sharding import PartitionSpec as P


def joined_along(blocks, dim):
    blocks = jnp.moveaxis(blocks, 0, dim)
    dims = blocks.shape
    return blocks.reshape(*dims[:dim], dims[dim] * dims[dim + 1], *dims[dim + 2 :])


def sent_to_all(x, axis):
    size = lax.axis_size(axis)
    return lax.all_to_all(jnp.broadcast_to(x[None], (size, *x.shape)), axis, 0, 0, tiled=True)


def gather_directly(x, axis, dim):
    return joined_along(sent_to_all(x, axis), dim)


def head_backward(pieces, query_pos, key_pos, scaling):
    queries, keys_all, values_all, grads_out, span, stride = pieces
    allowed = (query_pos[:, None] // span == key_pos[None, :] // span) & (
        (key_pos[None, :] - query_pos[:, None]) % stride == 0
    )
    scores = (
        jnp.einsum("qd,kd->qk", queries, keys_all, preferred_element_type=jnp.float32) * scaling
    )
    scores = jnp.where(allowed, scores, -1e30)
    shifted = jnp.exp(scores - jnp.max(scores, axis=1, keepdims=True))
    probs_full = shifted / jnp.sum(shifted, axis=1, keepdims=True)
    probs_half = probs_full.astype(jnp.bfloat16)
    head_out = jnp.einsum("qk,kd->qd", probs_half, values_all, preferred_element_type=jnp.float32)
    prob_grad = jnp.einsum("qd,kd->qk", grads_out, values_all, preferred_element_type=jnp.float32)
    row_delta = jnp.sum(probs_full * prob_grad, axis=1, keepdims=True)
    score_grad = (probs_full * (prob_grad - row_delta) * scaling).astype(jnp.bfloat16)
    query_grad = jnp.einsum("qk,kd->qd", score_grad, keys_all, preferred_element_type=jnp.float32)
    key_grad = jnp.einsum("qk,qd->kd", score_grad, queries, preferred_element_type=jnp.float32)
    value_grad = jnp.einsum("qk,qd->kd", probs_half, grads_out, preferred_element_type=jnp.float32)
    return (head_out, query_grad, key_grad, value_grad)


def local(
    tile_embed,
    qkv_saved,
    out_cotangent,
    qkv_weight,
    out_weight,
    seg_length,
    dilation,
    owner_map,
    tile_hidden,
    tile_output,
    embed_weight,
    proj_weight,
):
    head_count = seg_length.shape[0]
    heads_width = out_weight.shape[0]
    head_width = heads_width // head_count
    tokens_here = qkv_saved.shape[1]
    seq_count = lax.axis_size("seq")
    length = tokens_here * seq_count
    scaling = head_width ** (-0.5)
    saved = qkv_saved[0]
    cotangent = out_cotangent[0]
    embed_rows = tile_embed[0]

    def split_heads(block):
        return block.reshape(block.shape[0], head_count, head_width).transpose(1, 0, 2)

    def merge_heads(block):
        return block.transpose(1, 0, 2).reshape(block.shape[1], heads_width)

    key_value = gather_directly(saved[:, heads_width:], "seq", 0)
    grads_out = jnp.einsum(
        "td,cd->tc", cotangent, out_weight, preferred_element_type=jnp.float32
    ).astype(jnp.bfloat16)
    query_pos = lax.axis_index("seq") * tokens_here + jnp.arange(tokens_here, dtype=jnp.int32)
    key_pos = jnp.arange(length, dtype=jnp.int32)
    pieces = (
        split_heads(saved[:, :heads_width]),
        split_heads(key_value[:, :heads_width]),
        split_heads(key_value[:, heads_width:]),
        split_heads(grads_out),
        seg_length,
        dilation,
    )
    head_out, query_grad, key_grad, value_grad = lax.map(
        partial(head_backward, query_pos=query_pos, key_pos=key_pos, scaling=scaling), pieces
    )
    attention = merge_heads(head_out).astype(jnp.bfloat16)
    partials = jnp.concatenate([merge_heads(key_grad), merge_heads(value_grad)], axis=1)
    summed = lax.psum_scatter(
        partials.astype(jnp.bfloat16), "seq", scatter_dimension=0, tiled=True
    ).astype(jnp.float32)
    qkv_grad = jnp.concatenate([merge_heads(query_grad), summed], axis=1).astype(jnp.bfloat16)
    embed_grad = (
        cotangent.astype(jnp.float32)
        + jnp.einsum("tc,dc->td", qkv_grad, qkv_weight, preferred_element_type=jnp.float32)
    ).astype(jnp.bfloat16)
    columns = embed_rows
    qkv_sum = lax.psum_scatter(
        jnp.einsum("tc,tk->ck", columns, qkv_grad, preferred_element_type=jnp.float32),
        ("dp", "seq"),
        scatter_dimension=0,
        tiled=True,
    )
    columns = attention
    out_sum = lax.psum_scatter(
        jnp.einsum("tc,tk->ck", columns, cotangent, preferred_element_type=jnp.float32),
        ("dp", "seq"),
        scatter_dimension=0,
        tiled=True,
    )
    destination = owner_map[0, :, 0]
    capacity = tile_hidden.shape[1] // seq_count
    onehot = (destination[:, None] == jnp.arange(seq_count, dtype=jnp.int32)[None, :]).astype(
        jnp.int32
    )
    before = jnp.cumsum(onehot, axis=0) - onehot
    slot_index = destination * capacity + jnp.sum(before * onehot, axis=1)
    selector = (
        jnp.arange(seq_count * capacity, dtype=jnp.int32)[:, None] == slot_index[None, :]
    ).astype(jnp.bfloat16)
    outgoing = jnp.dot(selector, embed_grad, preferred_element_type=jnp.float32).astype(
        jnp.bfloat16
    )
    outgoing = outgoing.reshape(seq_count, capacity, embed_grad.shape[1])
    incoming = lax.all_to_all(outgoing, "seq", split_axis=0, concat_axis=0, tiled=True).reshape(
        seq_count * capacity, embed_grad.shape[1]
    )
    hidden_rows = tile_hidden[0]
    output_rows = tile_output[0]
    tile_grad = jnp.einsum("sd,ed->se", incoming, embed_weight, preferred_element_type=jnp.float32)
    grad_high = tile_grad.astype(jnp.bfloat16)
    hidden_grad = jnp.einsum(
        "se,fe->sf", grad_high, proj_weight, preferred_element_type=jnp.float32
    ).astype(jnp.bfloat16)[None]
    columns = output_rows
    embed_sum = lax.psum_scatter(
        jnp.einsum("sc,sd->cd", columns, incoming, preferred_element_type=jnp.float32),
        ("dp", "seq"),
        scatter_dimension=0,
        tiled=True,
    )
    columns = hidden_rows
    factor = lax.psum_scatter(
        jnp.einsum("sc,sd->cd", columns, incoming, preferred_element_type=jnp.float32),
        ("dp", "seq"),
        scatter_dimension=0,
        tiled=True,
    )
    proj_sum = jnp.dot(factor, embed_weight.astype(jnp.float32).T, precision=lax.Precision.HIGHEST)
    return (hidden_grad, proj_sum, embed_sum, qkv_sum, out_sum)


def solution(mesh):
    return jax.shard_map(
        local,
        mesh=mesh,
        in_specs=(
            P("dp", "seq", None),
            P("dp", "seq", None),
            P("dp", "seq", None),
            P(),
            P(),
            P(),
            P(),
            P("dp", "seq", None),
            P("dp", "seq", None),
            P("dp", "seq", None),
            P(),
            P(),
        ),
        out_specs=(
            P("dp", "seq", None),
            P(("dp", "seq"), None),
            P(("dp", "seq"), None),
            P(("dp", "seq"), None),
            P(("dp", "seq"), None),
        ),
        check_vma=False,
    )
```

profile of v0, /device:TPU:1, one launch (start us, length us, event | category | flops | bytes accessed | tf_op | source)
XLA Modules:
  0.0 817.1 jit_solution(7521575813613649928)
XLA Ops:
  8.5 4.1 broadcast_in_dim.57
  12.6 9.5 %all-to-all-start = ((bf16[32,128,768]{1,2,0:T(8,128)(2,1)}), bf16[32,128,768]{1,2,0:T(8,128)(2,1)}, u32[]{:S(2)}, u32[]{:S(2)}) async-start(bf16[32,128,768]{1,2,0:T(8,128)(2,1)} %broadcast_in_dim.57), calls=%async_computation | async-start | bytes 12582912 | tf_op jit(solution)/shard_map/all_to_all | solution.py:17
  23.7 85.8 %all-to-all-done = bf16[32,128,768]{1,2,0:T(8,128)(2,1)} async-done(((bf16[32,128,768]{1,2,0:T(8,128)(2,1)}), bf16[32,128,768]{1,2,0:T(8,128)(2,1)}, u32[]{:S(2)}, u32[]{:S(2)}) %all-to-all-start) | async-done | bytes 6291488 | tf_op jit(solution)/shard_map/all_to_all | solution.py:17
  109.5 3.7 copy_bitcast_fusion
  113.2 3.1 fusion.76
  116.3 288.8 %while.22 = (s32[]{:T(128)}, bf16[8,128,48]{1,2,0:T(8,128)(2,1)S(1)}, bf16[8,128,48]{1,2,0:T(8,128)(2,1)S(1)}, bf16[8,4096,48]{1,2,0:T(8,128)(2,1)}, bf16[8,4096...) while((s32[]{:T(128)}, ...), condition=%wide.region_6.7_spmd.clone.clone.clone, body=%wide.region_2.6_spmd.clone.clone.clone.sunk | while | flops 318800768 | bytes 23223004 | solution.py:91
  121.4 22.2 %fusion.110 = (f32[128]{0:T(128)S(1)}, f32[128,4096]{1,0:T(8,128)S(1)}) fusion(bf16[8,4096,48]{1,2,0:T(8,128)(2,1)} %get-tuple-element.522, s32[]{:T(128)} %get-tuple-element.500, bf16[8,128,48]{1,2,0:T(8,128)(2,1)S(1)} %get-tuple-element.521, pred[]{:T(512)S(6)} %lt.44, s32[]{:T(128)S(6)} %select_n.83, s32[128]{0:T(128)S(1)} %get-tuple-element.480, ...), kind=kOutput, calls=%fused_computation.101.clone.1 | convolution fusion | flops 57671552 | bytes 2521605 | tf_op jit(solution)/shard_map/while/body/eval_jaxpr/qd,kd->qk/dot_general | solution.py:30
  145.4 1.7 multiply_reduce_fusion.2
  156.7 22.2 %fusion.110 = (f32[128]{0:T(128)S(1)}, f32[128,4096]{1,0:T(8,128)S(1)}) fusion(bf16[8,4096,48]{1,2,0:T(8,128)(2,1)} %get-tuple-element.522, s32[]{:T(128)} %get-tuple-element.500, bf16[8,128,48]{1,2,0:T(8,128)(2,1)S(1)} %get-tuple-element.521, pred[]{:T(512)S(6)} %lt.44, s32[]{:T(128)S(6)} %select_n.83, s32[128]{0:T(128)S(1)} %get-tuple-element.480, ...), kind=kOutput, calls=%fused_computation.101.clone.1 | convolution fusion | flops 57671552 | bytes 2521605 | tf_op jit(solution)/shard_map/while/body/eval_jaxpr/qd,kd->qk/dot_general | solution.py:30
  180.7 1.7 multiply_reduce_fusion.2
  192.0 22.2 %fusion.110 = (f32[128]{0:T(128)S(1)}, f32[128,4096]{1,0:T(8,128)S(1)}) fusion(bf16[8,4096,48]{1,2,0:T(8,128)(2,1)} %get-tuple-element.522, s32[]{:T(128)} %get-tuple-element.500, bf16[8,128,48]{1,2,0:T(8,128)(2,1)S(1)} %get-tuple-element.521, pred[]{:T(512)S(6)} %lt.44, s32[]{:T(128)S(6)} %select_n.83, s32[128]{0:T(128)S(1)} %get-tuple-element.480, ...), kind=kOutput, calls=%fused_computation.101.clone.1 | convolution fusion | flops 57671552 | bytes 2521605 | tf_op jit(solution)/shard_map/while/body/eval_jaxpr/qd,kd->qk/dot_general | solution.py:30
  216.1 1.7 multiply_reduce_fusion.2
  227.4 22.2 %fusion.110 = (f32[128]{0:T(128)S(1)}, f32[128,4096]{1,0:T(8,128)S(1)}) fusion(bf16[8,4096,48]{1,2,0:T(8,128)(2,1)} %get-tuple-element.522, s32[]{:T(128)} %get-tuple-element.500, bf16[8,128,48]{1,2,0:T(8,128)(2,1)S(1)} %get-tuple-element.521, pred[]{:T(512)S(6)} %lt.44, s32[]{:T(128)S(6)} %select_n.83, s32[128]{0:T(128)S(1)} %get-tuple-element.480, ...), kind=kOutput, calls=%fused_computation.101.clone.1 | convolution fusion | flops 57671552 | bytes 2521605 | tf_op jit(solution)/shard_map/while/body/eval_jaxpr/qd,kd->qk/dot_general | solution.py:30
  262.6 22.2 %fusion.110 = (f32[128]{0:T(128)S(1)}, f32[128,4096]{1,0:T(8,128)S(1)}) fusion(bf16[8,4096,48]{1,2,0:T(8,128)(2,1)} %get-tuple-element.522, s32[]{:T(128)} %get-tuple-element.500, bf16[8,128,48]{1,2,0:T(8,128)(2,1)S(1)} %get-tuple-element.521, pred[]{:T(512)S(6)} %lt.44, s32[]{:T(128)S(6)} %select_n.83, s32[128]{0:T(128)S(1)} %get-tuple-element.480, ...), kind=kOutput, calls=%fused_computation.101.clone.1 | convolution fusion | flops 57671552 | bytes 2521605 | tf_op jit(solution)/shard_map/while/body/eval_jaxpr/qd,kd->qk/dot_general | solution.py:30
  297.9 22.2 %fusion.110 = (f32[128]{0:T(128)S(1)}, f32[128,4096]{1,0:T(8,128)S(1)}) fusion(bf16[8,4096,48]{1,2,0:T(8,128)(2,1)} %get-tuple-element.522, s32[]{:T(128)} %get-tuple-element.500, bf16[8,128,48]{1,2,0:T(8,128)(2,1)S(1)} %get-tuple-element.521, pred[]{:T(512)S(6)} %lt.44, s32[]{:T(128)S(6)} %select_n.83, s32[128]{0:T(128)S(1)} %get-tuple-element.480, ...), kind=kOutput, calls=%fused_computation.101.clone.1 | convolution fusion | flops 57671552 | bytes 2521605 | tf_op jit(solution)/shard_map/while/body/eval_jaxpr/qd,kd->qk/dot_general | solution.py:30
  321.9 1.7 multiply_reduce_fusion.2
  333.2 22.2 %fusion.110 = (f32[128]{0:T(128)S(1)}, f32[128,4096]{1,0:T(8,128)S(1)}) fusion(bf16[8,4096,48]{1,2,0:T(8,128)(2,1)} %get-tuple-element.522, s32[]{:T(128)} %get-tuple-element.500, bf16[8,128,48]{1,2,0:T(8,128)(2,1)S(1)} %get-tuple-element.521, pred[]{:T(512)S(6)} %lt.44, s32[]{:T(128)S(6)} %select_n.83, s32[128]{0:T(128)S(1)} %get-tuple-element.480, ...), kind=kOutput, calls=%fused_computation.101.clone.1 | convolution fusion | flops 57671552 | bytes 2521605 | tf_op jit(solution)/shard_map/while/body/eval_jaxpr/qd,kd->qk/dot_general | solution.py:30
  357.2 1.7 multiply_reduce_fusion.2
  368.5 22.2 %fusion.110 = (f32[128]{0:T(128)S(1)}, f32[128,4096]{1,0:T(8,128)S(1)}) fusion(bf16[8,4096,48]{1,2,0:T(8,128)(2,1)} %get-tuple-element.522, s32[]{:T(128)} %get-tuple-element.500, bf16[8,128,48]{1,2,0:T(8,128)(2,1)S(1)} %get-tuple-element.521, pred[]{:T(512)S(6)} %lt.44, s32[]{:T(128)S(6)} %select_n.83, s32[128]{0:T(128)S(1)} %get-tuple-element.480, ...), kind=kOutput, calls=%fused_computation.101.clone.1 | convolution fusion | flops 57671552 | bytes 2521605 | tf_op jit(solution)/shard_map/while/body/eval_jaxpr/qd,kd->qk/dot_general | solution.py:30
  392.5 1.7 multiply_reduce_fusion.2
  405.2 6.3 pad_maximum_fusion
  411.5 8.7 %copy.37 = bf16[4096,768]{1,0:T(8,128)(2,1)} copy(bf16[4096,768]{0,1:T(8,128)(2,1)} %pad_maximum_fusion) | data formatting | bytes 12582912
  421.2 157.9 %reduce-scatter.7.cloned.1.call-done = bf16[128,768]{1,0:T(8,128)(2,1)} async-done(((bf16[4096,768]{1,0:T(8,128)(2,1)}), bf16[128,768]{1,0:T(8,128)(2,1)}) %reduce-scatter.7.cloned.1.call-update) | async-done | bytes 196624
  580.2 3.2 fusion.53
  583.4 4.5 all-to-all-start.1
  589.2 2.4 convolution_bitcast_fusion.4
  591.7 5.9 all-to-all-done.1
  597.6 4.1 convolution_bitcast_fusion.5
  601.6 3.0 convolution_bitcast_fusion.6
  604.7 5.3 fusion.52
  610.0 190.4 %all-reduce.7.cloned.1.call-done = (f32[1536,768]{0,1:T(8,128)}, f32[1536,768]{0,1:T(8,128)}, f32[768,1152]{0,1:T(8,128)}, f32[384,768]{1,0:T(8,128)}) async-done(((f32[1536,768]{0,1:T(8,128)}, f32[1536,768]{0,1:T(8,128)}, f32[768,1152]{0,1:T(8,128)}, f32[384,768]{1,0:T(8,128)}), (f32[1536,768]{0,1:T(8,128)}, f32[1536,768]{0,1:T(8,128)}, f32[768,1152]{0,1:T(8,128)}, ...) | async-done | bytes 14155792
  804.7 3.9 fusion.57
  (128 shorter events, 91.2 us)
Async XLA Ops:
  7.2 597.6 %copy-start = (bf16[1536,768]{1,0:T(8,128)(2,1)S(1)}, bf16[1536,768]{1,0:T(8,128)(2,1)}, u32[]{:S(2)}) copy-start(bf16[1536,768]{1,0:T(8,128)(2,1)} %param.24) | copy-start | bytes 7077892
  12.6 9.6 %copy-start.1 = (bf16[1,128,768]{2,1,0:T(8,128)(2,1)S(1)}, bf16[1,128,768]{2,1,0:T(8,128)(2,1)}, u32[]{:S(2)}) copy-start(bf16[1,128,768]{2,1,0:T(8,128)(2,1)} %param.16) | copy-start | bytes 589828
  12.6 96.9 %all-to-all-start = ((bf16[32,128,768]{1,2,0:T(8,128)(2,1)}), bf16[32,128,768]{1,2,0:T(8,128)(2,1)}, u32[]{:S(2)}, u32[]{:S(2)}) async-start(bf16[32,128,768]{1,2,0:T(8,128)(2,1)} %broadcast_in_dim.57), calls=%async_computation | async-start | bytes 12582912 | tf_op jit(solution)/shard_map/all_to_all | solution.py:17
  22.1 557.0 %reduce-scatter.7.cloned.1.call-start = ((), (), s32[]{:S(2)}) async-start(), calls=%async_computation.3 | async-start | bytes 6488064
  113.2 3.1 copy-start.5
  113.2 3.1 copy-start.6
  420.1 0.7 copy-start.4
  580.2 9.1 %copy-start.3 = (bf16[1,128,768]{2,1,0:T(8,128)(2,1)S(1)}, bf16[1,128,768]{2,1,0:T(8,128)(2,1)}, u32[]{:S(2)}) copy-start(bf16[1,128,768]{2,1,0:T(8,128)(2,1)} %param.14) | copy-start | bytes 589828
  583.4 14.2 %all-to-all-start.1 = ((bf16[32,8,768]{2,1,0:T(8,128)(2,1)}), bf16[32,8,768]{2,1,0:T(8,128)(2,1)S(1)}, u32[]{:S(2)}, u32[]{:S(2)}) async-start(bf16[32,8,768]{2,1,0:T(8,128)(2,1)} %fusion.53), calls=%async_computation.1 | async-start | bytes 786432 | tf_op jit(solution)/shard_map/all_to_all | solution.py:132
  587.9 212.5 %all-reduce.7.cloned.1.call-start = ((), (), s32[]{:S(2)}) async-start(), calls=%async_computation.4 | async-start | bytes 28311552
  591.7 10.0 %copy-start.2 = (bf16[1,256,1536]{2,1,0:T(8,128)(2,1)S(1)}, bf16[1,256,1536]{2,1,0:T(8,128)(2,1)}, u32[]{:S(2)}) copy-start(bf16[1,256,1536]{2,1,0:T(8,128)(2,1)} %param.22) | copy-start | bytes 2359300
Sparse Core Ops, SparseCore 0:
  420.3 158.7 reduce-scatter.6
  604.8 195.4 all-reduce.6
where the time goes:
time: 828 us; the launch traced here: 817 us
  waiting for transfers between devices  440 us (53%)
  matrix products  259 us (31%)
  local copies, waits for them, and re-layouts  37.9 us (5%)
  other arithmetic  29.4 us (4%)
  loops' own time  22.3 us (3%)
  between operations  14.4 us (2%)
  starting transfers between devices  14 us (2%)
    unnamed x4, waiting for transfers between devices  348 us
    dot_general x8, matrix products, head_backward(): jnp.einsum('qd,kd->qk', queries, keys_all, preferred_element_type=jnp.flo...  178 us
    all_to_all x1, waiting for transfers between devices, sent_to_all(): lax.all_to_all(jnp.broadcast_to(x[None], (size, *x.shape)), axis, 0, 0, t...  85.8 us
    another operation x1, loops' own time, local(): lax.map(partial(head_backward, query_pos=query_pos, key_pos=key_pos, scal...  22.3 us
    unnamed x22, local copies, waits for them, and re-layouts  17.5 us
  transfers between devices with their start and end apart: 4, of which 4 were waited for; matrix products, arithmetic and copies ran while one was open for 1% of the time, Pallas kernels for 0%

commit v1 on v0

v1 whole, which is shorter than its diff:
```python
from functools import partial

import jax
import jax.numpy as jnp
from jax import lax
from jax.experimental import pallas as pl
from jax.experimental.pallas import tpu as pltpu
from jax.sharding import Mesh, PartitionSpec as P

F32 = jnp.float32
BF16 = jnp.bfloat16
DP = ("zh", "co")
SEQ = ("y", "x", "zl")
GRP = ("x", "zl")
ALL = DP + SEQ
QB = 256
KC = 512
LOG2E = 1.4426950408889634


def exchange(x, axes):
    return lax.all_to_all(x, axes, 0, 0, tiled=True)


def sent_to_all(x, axes):
    n = lax.axis_size(axes)
    return exchange(jnp.broadcast_to(x[None], (n, *x.shape)), axes)


def attention_kernel(
    par, kv, qd, dkv, qo, kmat, vmat, kt, vt, code, score, prob, dk, dv, *, hd, tok, nkb, scaling
):
    step = pl.program_id(0)
    length = nkb * tok
    off = par[0]
    inv_len, dil, inv_dil = par[1], par[2], par[3]

    def code_of(pos):
        seg = jnp.floor((pos + 0.5) * inv_len)
        res = pos - dil * jnp.floor((pos + 0.5) * inv_dil)
        return seg * 8.0 + res

    @pl.when(step == 0)
    def _():
        for b in range(nkb):
            kb = kv[b, :hd, :]
            vb = kv[b, hd:, :]
            kt[:, b * tok : (b + 1) * tok] = kb
            vt[:, b * tok : (b + 1) * tok] = vb
            kmat[b * tok : (b + 1) * tok, :] = kb.astype(F32).T.astype(BF16)
            vmat[b * tok : (b + 1) * tok, :] = vb.astype(F32).T.astype(BF16)
            pos = lax.broadcasted_iota(jnp.int32, (tok, 128), 0).astype(F32) + float(b * tok)
            code[b * tok : (b + 1) * tok, :] = code_of(pos)
        dk[...] = jnp.zeros_like(dk)
        dv[...] = jnp.zeros_like(dv)

    nb = QB // tok
    qt = jnp.concatenate([qd[b, :hd, :] for b in range(nb)], axis=1)
    dot_ = jnp.concatenate([qd[b, hd:, :] for b in range(nb)], axis=1).astype(F32)
    qpos = lax.broadcasted_iota(jnp.int32, (8, QB), 1).astype(F32) + off + (step * QB).astype(F32)
    qcode = code_of(qpos)[0:1, :]

    mx = jnp.full((8, QB), -3e38, F32)
    for c in range(length // KC):
        rows = slice(c * KC, (c + 1) * KC)
        s = jnp.dot(kmat[rows, :], qt, preferred_element_type=F32)
        ck = code[rows, :]
        s = jnp.where(jnp.concatenate([ck] * (QB // 128), axis=1) == qcode, s, -1e30)
        score[rows, :] = s
        mx = jnp.maximum(mx, jnp.max(s.reshape(KC // 8, 8, QB), axis=0))
    top = jnp.max(mx, axis=0, keepdims=True)

    tot = jnp.zeros((8, QB), F32)
    ot = jnp.zeros((hd, QB), F32)
    for c in range(length // KC):
        rows = slice(c * KC, (c + 1) * KC)
        p = jnp.exp2((score[rows, :] - top) * (scaling * LOG2E))
        tot = tot + jnp.sum(p.reshape(KC // 8, 8, QB), axis=0)
        ph = p.astype(BF16)
        prob[rows, :] = ph
        ot = ot + jnp.dot(vt[:, rows], ph, preferred_element_type=F32)
    inv = 1.0 / jnp.sum(tot, axis=0, keepdims=True)
    ot = ot * inv
    dn = dot_ * inv
    dnh = dn.astype(BF16)
    delta = jnp.sum(dnh.astype(F32) * ot, axis=0, keepdims=True)
    dmat = dn.T.astype(BF16)
    qmat = qt.astype(F32).T.astype(BF16)

    dqt = jnp.zeros((hd, QB), F32)
    for c in range(length // KC):
        rows = slice(c * KC, (c + 1) * KC)
        ph = prob[rows, :]
        dp = jnp.dot(vmat[rows, :], dnh, preferred_element_type=F32)
        ds = (ph.astype(F32) * (dp - delta)).astype(BF16)
        dv[rows, :] += jnp.dot(ph, dmat, preferred_element_type=F32)
        dk[rows, :] += jnp.dot(ds, qmat, preferred_element_type=F32)
        dqt = dqt + jnp.dot(kt[:, rows], ds, preferred_element_type=F32)

    for b in range(nb):
        cols = slice(b * tok, (b + 1) * tok)
        qo[b, :hd, :] = (dqt[:, cols] * scaling).astype(BF16)
        qo[b, hd:, :] = ot[:, cols].astype(BF16)

    @pl.when(step == pl.num_programs(0) - 1)
    def _():
        for b in range(nkb):
            rows = slice(b * tok, (b + 1) * tok)
            dkv[b, :hd, :] = (dk[rows, :].T * scaling).astype(BF16)
            dkv[b, hd:, :] = dv[rows, :].T.astype(BF16)


def attention_grads(par, kv, qd, scaling):
    nkb, two, tok = kv.shape
    hd = two // 2
    nqb = qd.shape[0]
    length = nkb * tok
    steps = nqb * tok // QB
    nb = QB // tok
    return pl.pallas_call(
        partial(attention_kernel, hd=hd, tok=tok, nkb=nkb, scaling=scaling),
        grid=(steps,),
        out_shape=(
            jax.ShapeDtypeStruct((nkb, two, tok), BF16),
            jax.ShapeDtypeStruct((nqb, two, tok), BF16),
        ),
        in_specs=[
            pl.BlockSpec(memory_space=pltpu.SMEM),
            pl.BlockSpec((nkb, two, tok), lambda i: (0, 0, 0)),
            pl.BlockSpec((nb, two, tok), lambda i: (i, 0, 0)),
        ],
        out_specs=(
            pl.BlockSpec((nkb, two, tok), lambda i: (0, 0, 0)),
            pl.BlockSpec((nb, two, tok), lambda i: (i, 0, 0)),
        ),
        scratch_shapes=[
            pltpu.VMEM((length, hd), BF16),
            pltpu.VMEM((length, hd), BF16),
            pltpu.VMEM((hd, length), BF16),
            pltpu.VMEM((hd, length), BF16),
            pltpu.VMEM((length, 128), F32),
            pltpu.VMEM((length, QB), F32),
            pltpu.VMEM((length, QB), BF16),
            pltpu.VMEM((length, hd), F32),
            pltpu.VMEM((length, hd), F32),
        ],
        compiler_params=pltpu.CompilerParams(dimension_semantics=("arbitrary",)),
        cost_estimate=pl.CostEstimate(
            flops=30_000_000_000, bytes_accessed=4_000_000, transcendentals=length * nqb * tok
        ),
        name="attention_grads",
    )(par, kv, qd)


def local(
    tile_embed,
    qkv_saved,
    out_cotangent,
    qkv_weight,
    out_weight,
    seg_length,
    dilation,
    owner_map,
    tile_hidden,
    tile_output,
    embed_weight,
    proj_weight,
):
    heads = seg_length.shape[0]
    width = out_weight.shape[0]
    hd = width // heads
    tok = qkv_saved.shape[1]
    d_slide = tile_embed.shape[2]
    n_seq = lax.axis_size(SEQ)
    n_y = lax.axis_size("y")
    n_grp = lax.axis_size(GRP)
    n_dp = lax.axis_size(DP)
    n_dev = n_dp * n_seq
    scaling = hd ** (-0.5)
    cot = out_cotangent[0]
    head = lax.axis_index(GRP)
    core = lax.axis_index("co")

    saved_t = qkv_saved[0].T.reshape(3, heads, hd, tok)
    grads_t = jnp.einsum("cd,td->ct", out_weight, cot, preferred_element_type=F32)
    grads_t = grads_t.astype(BF16).reshape(heads, hd, tok)
    outgoing = jnp.concatenate([saved_t[0], grads_t, saved_t[1], saved_t[2]], axis=1)
    mine = exchange(outgoing, GRP)
    qd = mine[:, : 2 * hd]
    kv = sent_to_all(mine[:, 2 * hd :], "y").reshape(n_seq, 2 * hd, tok)

    seg = seg_length[head].astype(F32)
    dil = dilation[head].astype(F32)
    off = (lax.axis_index("y") * n_grp * tok).astype(F32)
    par = jnp.stack([off, 1.0 / seg, dil, 1.0 / dil])
    dkv, qo = attention_grads(par, kv, qd, scaling)

    embed_all = sent_to_all(tile_embed[0], GRP).reshape(n_grp * tok, d_slide)
    pick = jnp.where(core == 0, tile_hidden[0], tile_output[0])
    keep = jnp.where(core == 0, tile_output[0], tile_hidden[0])
    other = lax.ppermute(pick, "co", [(0, 1), (1, 0)])

    terms = exchange(dkv.reshape(n_y, n_grp, 2 * hd, tok), "y")
    dkv_sum = jnp.sum(terms.astype(F32), axis=0).astype(BF16)
    back = jnp.concatenate([qo, dkv_sum], axis=1)
    got = exchange(back, GRP)

    grad_t = jnp.concatenate([qo[:, :hd], dkv_sum], axis=1).transpose(1, 0, 2)
    grad_t = grad_t.reshape(3 * hd, n_grp * tok)
    qkv_term = jnp.einsum("td,ct->dc", embed_all, grad_t, preferred_element_type=F32)
    qkv_term = qkv_term.astype(BF16).reshape(n_dp * n_y, -1, 3 * hd)
    qkv_part = jnp.sum(exchange(qkv_term, DP + ("y",)).astype(F32), axis=0)
    qkv_part = exchange(qkv_part.reshape(n_grp, -1, 3 * hd), GRP)
    rows = qkv_part.shape[1]
    qkv_sum = qkv_part.reshape(heads, rows, 3, hd).transpose(1, 2, 0, 3).reshape(rows, 3 * width)

    got = got.reshape(heads, 4, hd, tok)
    attention_t = got[:, 1].reshape(width, tok)
    qkv_grad_t = jnp.concatenate([got[:, 0], got[:, 2], got[:, 3]], axis=0).reshape(3 * width, tok)
    out_term = jnp.einsum("ct,td->cd", attention_t, cot, preferred_element_type=F32)
    out_term = out_term.astype(BF16).reshape(n_dev, -1, d_slide)
    out_sum = jnp.sum(exchange(out_term, ALL).astype(F32), axis=0)

    embed_grad = (
        cot.astype(F32)
        + jnp.einsum("ct,dc->td", qkv_grad_t, qkv_weight, preferred_element_type=F32)
    ).astype(BF16)

    destination = owner_map[0, :, 0]
    capacity = tile_hidden.shape[1] // n_seq
    onehot = (destination[:, None] == jnp.arange(n_seq, dtype=jnp.int32)[None, :]).astype(F32)
    lower = (
        jnp.arange(tok, dtype=jnp.int32)[:, None] > jnp.arange(tok, dtype=jnp.int32)[None, :]
    ).astype(BF16)
    before = jnp.dot(lower, onehot.astype(BF16), preferred_element_type=F32)
    rank = jnp.sum(before * onehot, axis=1).astype(jnp.int32)
    slot_index = destination * capacity + rank
    selector = (
        jnp.arange(n_seq * capacity, dtype=jnp.int32)[:, None] == slot_index[None, :]
    ).astype(BF16)
    routed = jnp.dot(selector, embed_grad, preferred_element_type=F32).astype(BF16)
    incoming = exchange(routed.reshape(n_seq, capacity, d_slide), SEQ).reshape(-1, d_slide)

    swapped = lax.ppermute(incoming, "co", [(0, 1), (1, 0)])
    term = jnp.einsum("sc,sd->cd", keep, incoming, preferred_element_type=F32)
    term = term + jnp.einsum("sc,sd->cd", other, swapped, preferred_element_type=F32)
    n_zh = lax.axis_size("zh")
    d_tile = embed_weight.shape[0]
    per = d_tile // n_dev
    term = term.astype(BF16).reshape(n_zh, 2, n_seq, per, d_slide).transpose(0, 2, 1, 3, 4)
    term = exchange(term.reshape(n_zh * n_seq, 2, per, d_slide), ("zh",) + SEQ)
    both = exchange(jnp.sum(term.astype(F32), axis=0), "co")
    embed_sum = both[0]
    factor = both[1]

    tile_grad = jnp.einsum("sd,ed->se", incoming, embed_weight, preferred_element_type=F32)
    hidden_grad = jnp.einsum(
        "se,fe->sf", tile_grad.astype(BF16), proj_weight, preferred_element_type=F32
    ).astype(BF16)[None]
    proj_sum = jnp.dot(factor, embed_weight.astype(F32).T, precision=lax.Precision.HIGHEST)
    return (hidden_grad, proj_sum, embed_sum, qkv_sum, out_sum)


def solution(mesh):
    fine = Mesh(mesh.devices.reshape(2, 2, 4, 4, 2), ALL)
    part = P(DP, SEQ, None)
    rows = P(ALL, None)
    return jax.shard_map(
        local,
        mesh=fine,
        in_specs=(part, part, part, P(), P(), P(), P(), part, part, part, P(), P()),
        out_specs=(part, rows, rows, rows, rows),
        check_vma=False,
    )
```

time: 828 us -> 226 us (0.27); the launches traced: 817 us -> 224 us
  waiting for transfers between devices: 440 us -> 58.5 us
  matrix products: 259 us -> 21.3 us
  starting transfers between devices: 14 us -> 54.4 us
  blocking collectives: 0 us -> 30.4 us
  loops' own time: 22.3 us -> 0 us
  Pallas kernels: 0 us -> 21.2 us
  other arithmetic: 29.4 us -> 11.5 us
  local copies, waits for them, and re-layouts: 37.9 us -> 24.8 us
  between operations: 14.4 us -> 2.3 us
    unnamed x4 -> x0, waiting for transfers between devices: 348 us -> none
    dot_general x56 -> x9, matrix products: 259 us -> 21.3 us  [the longest x1 5.38 us: local(): jnp.einsum('se,fe->sf', tile_grad.astype(BF16), proj_weight, preferred_el...]
    all_to_all x2 -> x8, starting transfers between devices: 14 us -> 49.9 us  [exchange(): return lax.all_to_all(x, axes, 0, 0, tiled=True)]
    all_to_all x2 -> x8, waiting for transfers between devices: 91.7 us -> 58.5 us  [exchange(): return lax.all_to_all(x, axes, 0, 0, tiled=True)]
    all_to_all x0 -> x3, blocking collectives: none -> 30.4 us  [exchange(): return lax.all_to_all(x, axes, 0, 0, tiled=True)]
    another operation x1 -> x0, loops' own time: 22.3 us -> none  [local(): lax.map(partial(head_backward, query_pos=query_pos, key_pos=key_pos, scal...]
    pallas_call x0 -> x1, Pallas kernels: none -> 21.2 us  [attention_grads(): pl.pallas_call(partial(attention_kernel, hd=hd, tok=tok, nkb=nkb, scaling...]
    unnamed x22, local copies, waits for them, and re-layouts: 17.5 us -> 1.73 us
  transfers between devices with their start and end apart: 4 -> 10, of which waited for: 4 -> 6; matrix products, arithmetic and copies ran while one was open for 1% -> 20% of each run, Pallas kernels for 0% -> 0%
where the time goes in v1:
time: 226 us; the launch traced here: 224 us
  waiting for transfers between devices  58.5 us (26%)
  starting transfers between devices  54.4 us (24%)
  blocking collectives  30.4 us (13%)
  local copies, waits for them, and re-layouts  24.8 us (11%)
  matrix products  21.3 us (9%)
  Pallas kernels  21.2 us (9%)
  other arithmetic  11.5 us (5%)
  between operations  2.3 us (1%)
    all_to_all x8, waiting for transfers between devices, exchange(): return lax.all_to_all(x, axes, 0, 0, tiled=True)  58.5 us
    all_to_all x8, starting transfers between devices, exchange(): return lax.all_to_all(x, axes, 0, 0, tiled=True)  49.9 us
    all_to_all x3, blocking collectives, exchange(): return lax.all_to_all(x, axes, 0, 0, tiled=True)  30.4 us
    pallas_call x1, Pallas kernels, attention_grads(): pl.pallas_call(partial(attention_kernel, hd=hd, tok=tok, nkb=nkb, scaling...  21.2 us
    dot_general x1, matrix products, local(): jnp.einsum('se,fe->sf', tile_grad.astype(BF16), proj_weight, preferred_el...  5.38 us
    reshape x1, local copies, waits for them, and re-layouts, local(): term.astype(BF16).reshape(n_zh, 2, n_seq, per, d_slide)  4.87 us
  transfers between devices with their start and end apart: 10, of which 6 were waited for; matrix products, arithmetic and copies ran while one was open for 20% of the time, Pallas kernels for 0%

profile of v1, /device:TPU:1, one launch (start us, length us, event | category | flops | bytes accessed | tf_op | source)
XLA Modules:
  0.0 224.5 jit_solution(6553334903527020090)
XLA Ops:
  3.7 13.3 %all_to_all.55 = bf16[8,192,128]{2,1,0:T(8,128)(2,1)S(1)} all-to-all(bf16[8,192,128]{2,1,0:T(8,128)(2,1)S(1)} %pad_maximum_fusion), channel_id=1, replica_groups=mesh['zh'=2,'co'=2,'y'=4,'x'=4,'zl'=2] {'x','zl'}, dimensions={0} | all-to-all | bytes 786432 | tf_op jit(solution)/shard_map/all_to_all | solution.py:22
  18.7 4.2 %all-to-all-start.1 = ((bf16[4,8,96,128]{3,2,1,0:T(8,128)(2,1)}), bf16[4,8,96,128]{3,2,1,0:T(8,128)(2,1)S(1)}, u32[]{:S(2)}, u32[]{:S(2)}) async-start(bf16[4,8,96,128]{3,2,1,0:T(8,128)(2,1)} %broadcast_in_dim.8), calls=%async_computation.1 | async-start | bytes 1572864 | tf_op jit(solution)/shard_map/all_to_all | solution.py:22
  26.0 6.5 %all-to-all-done.1 = bf16[4,8,96,128]{3,2,1,0:T(8,128)(2,1)S(1)} async-done(((bf16[4,8,96,128]{3,2,1,0:T(8,128)(2,1)}), bf16[4,8,96,128]{3,2,1,0:T(8,128)(2,1)S(1)}, u32[]{:S(2)}, u32[]{:S(2)}) %all-to-all-start.1) | async-done | bytes 786464 | tf_op jit(solution)/shard_map/all_to_all | solution.py:22
  33.4 21.2 %attention_grads.1 = (bf16[32,96,128]{2,1,0:T(8,128)(2,1)}, bf16[8,96,128]{2,1,0:T(8,128)(2,1)}) custom-call(f32[4]{0:T(128)} %pad_maximum_fusion.3.par, bf16[32,96,128]{2,1,0:T(8,128)(2,1)} %bitcast.88, bf16[8,96,128]{2,1,0:T(8,128)(2,1)} %get-tuple-element.13.qd), custom_call_target="tpu_custom_call" | custom-call | flops 30000001024 | bytes 4000000 | tf_op jit(solution)/shard_map/attention_grads/pallas_call | solution.py:120
  54.6 11.9 %all_to_all.56 = bf16[4,8,96,128]{3,2,1,0:T(8,128)(2,1)S(1)} all-to-all(bf16[4,8,96,128]{3,2,1,0:T(8,128)(2,1)} %bitcast.89), channel_id=1, replica_groups=mesh['zh'=2,'co'=2,'y'=4,'x'=4,'zl'=2] {'y'}, dimensions={0} | all-to-all | bytes 1572864 | tf_op jit(solution)/shard_map/all_to_all | solution.py:22
  67.8 4.5 %all-to-all-start.7 = ((bf16[8,128,768]{2,1,0:T(8,128)(2,1)}), bf16[8,128,768]{2,1,0:T(8,128)(2,1)}, u32[]{:S(2)}, u32[]{:S(2)}) async-start(bf16[8,128,768]{2,1,0:T(8,128)(2,1)} %broadcast_in_dim.11), calls=%async_computation.7 | async-start | bytes 3145728 | tf_op jit(solution)/shard_map/all_to_all | solution.py:22
  73.3 18.2 %all-to-all-done.7 = bf16[8,128,768]{2,1,0:T(8,128)(2,1)} async-done(((bf16[8,128,768]{2,1,0:T(8,128)(2,1)}), bf16[8,128,768]{2,1,0:T(8,128)(2,1)}, u32[]{:S(2)}, u32[]{:S(2)}) %all-to-all-start.7) | async-done | bytes 1572896 | tf_op jit(solution)/shard_map/all_to_all | solution.py:22
  91.5 4.5 %all-to-all-start.3 = ((bf16[8,192,128]{2,1,0:T(8,128)(2,1)}), bf16[8,192,128]{2,1,0:T(8,128)(2,1)S(1)}, u32[]{:S(2)}, u32[]{:S(2)}) async-start(bf16[8,192,128]{2,1,0:T(8,128)(2,1)} %pad_maximum_fusion.1), calls=%async_computation.3 | async-start | bytes 786432 | tf_op jit(solution)/shard_map/all_to_all | solution.py:22
  96.0 1.9 fusion.4
  98.8 3.5 %all-to-all-done.3 = bf16[8,192,128]{2,1,0:T(8,128)(2,1)S(1)} async-done(((bf16[8,192,128]{2,1,0:T(8,128)(2,1)}), bf16[8,192,128]{2,1,0:T(8,128)(2,1)S(1)}, u32[]{:S(2)}, u32[]{:S(2)}) %all-to-all-start.3) | async-done | bytes 393248 | tf_op jit(solution)/shard_map/all_to_all | solution.py:22
  102.3 9.6 %all-to-all-start.8 = ((bf16[16,48,144]{2,1,0:T(8,128)(2,1)}), bf16[16,48,144]{2,1,0:T(8,128)(2,1)}, u32[]{:S(2)}, u32[]{:S(2)}) async-start(bf16[16,48,144]{2,1,0:T(8,128)(2,1)} %bitcast.30), calls=%async_computation.8 | async-start | bytes 786432 | tf_op jit(solution)/shard_map/all_to_all | solution.py:22
  113.9 3.3 %fusion.1 = bf16[32,8,768]{2,1,0:T(8,128)(2,1)} fusion(bf16[1152,128]{1,0:T(8,128)(2,1)} %bitcast.87, bf16[768,1152]{1,0:T(8,128)(2,1)} %param.15, bf16[1,128,768]{2,1,0:T(8,128)(2,1)S(1)} %copy-done.2, s32[128]{0:T(128)S(1)} %convert_add_fusion), kind=kOutput, calls=%fused_computation.9 | convolution fusion | flops 277348352 | bytes 2654720 | tf_op jit(solution)/shard_map/dot_general | solution.py:241
  117.1 4.5 %all-to-all-done.8 = bf16[16,48,144]{2,1,0:T(8,128)(2,1)} async-done(((bf16[16,48,144]{2,1,0:T(8,128)(2,1)}), bf16[16,48,144]{2,1,0:T(8,128)(2,1)}, u32[]{:S(2)}, u32[]{:S(2)}) %all-to-all-start.8) | async-done | bytes 221216 | tf_op jit(solution)/shard_map/all_to_all | solution.py:22
  121.6 4.6 %all-to-all-start.4 = ((bf16[32,8,768]{2,1,0:T(8,128)(2,1)}), bf16[32,8,768]{2,1,0:T(8,128)(2,1)}, u32[]{:S(2)}, u32[]{:S(2)}) async-start(bf16[32,8,768]{2,1,0:T(8,128)(2,1)} %fusion.1), calls=%async_computation.4 | async-start | bytes 786432 | tf_op jit(solution)/shard_map/all_to_all | solution.py:22
  127.2 2.4 %collective-permute-start = (bf16[256,1536]{1,0:T(8,128)(2,1)}, bf16[256,1536]{1,0:T(8,128)(2,1)}, u32[]{:S(2)}, u32[]{:S(2)}) collective-permute-start(bf16[256,1536]{1,0:T(8,128)(2,1)} %select_bitcast_fusion), channel_id=1, source_target_pairs={{0,32},{32,0},{1,33},{33,1},{2,34},{34,2},{3,35},{35,3},{4,36},{36... | collective-permute-start | bytes 2359304 | tf_op jit(solution)/shard_map/ppermute | solution.py:201
  131.4 4.5 %all-to-all-done.4 = bf16[32,8,768]{2,1,0:T(8,128)(2,1)} async-done(((bf16[32,8,768]{2,1,0:T(8,128)(2,1)}), bf16[32,8,768]{2,1,0:T(8,128)(2,1)}, u32[]{:S(2)}, u32[]{:S(2)}) %all-to-all-start.4) | async-done | bytes 393248 | tf_op jit(solution)/shard_map/all_to_all | solution.py:22
  135.8 4.0 %all-to-all-start.9 = ((f32[8,1,864]{2,1,0:T(1,128)}), f32[8,1,864]{2,1,0:T(1,128)}, u32[]{:S(2)}, u32[]{:S(2)}) async-start(f32[8,1,864]{2,1,0:T(1,128)} %reshape.99), calls=%async_computation.9 | async-start | bytes 57344 | tf_op jit(solution)/shard_map/all_to_all | solution.py:22
  140.9 2.0 reshape.97
  142.9 2.1 collective-permute-start.1
  145.1 7.7 %all-to-all-start.10 = ((bf16[128,3,768]{2,1,0:T(4,128)(2,1)}), bf16[128,3,768]{2,1,0:T(4,128)(2,1)}, u32[]{:S(2)}, u32[]{:S(2)}) async-start(bf16[128,3,768]{2,1,0:T(4,128)(2,1)} %reshape.97), calls=%async_computation.10 | async-start | bytes 1572864 | tf_op jit(solution)/shard_map/all_to_all | solution.py:22
  152.8 2.1 fusion.6
  154.9 3.4 %add_convert_fusion = bf16[1536,768]{1,0:T(8,128)(2,1)} fusion(f32[1536,768]{1,0:T(8,128)S(1)} %fusion.6, bf16[256,1536]{1,0:T(8,128)(2,1)} %collective-permute-done, bf16[256,768]{1,0:T(8,128)(2,1)S(1)} %collective-permute-done.1), kind=kOutput, calls=%fused_computation.1 | convolution fusion | flops 606339072 | bytes 8257536 | tf_op jit(solution)/shard_map/sc,sd->cd/dot_general | solution.py:246
  158.3 4.9 %reshape.91 = bf16[2,2,32,12,768]{4,3,2,1,0:T(8,128)(2,1)} reshape(bf16[1536,768]{1,0:T(8,128)(2,1)} %add_convert_fusion) | data formatting | bytes 4718592 | tf_op jit(solution)/shard_map/reshape | solution.py:250
  163.2 2.6 %copy.74 = bf16[2,32,2,12,768]{4,1,0,3,2:T(8,128)(2,1)S(1)} copy(bf16[2,32,2,12,768]{4,3,1,2,0:T(8,128)(2,1)} %bitcast.84) | data formatting | bytes 4718592 | tf_op jit(solution)/shard_map/transpose | solution.py:250
  165.8 3.9 %copy.75 = bf16[64,2,12,768]{3,1,2,0:T(2,128)(2,1)} copy(bf16[64,2,12,768]{3,0,2,1:T(8,128)(2,1)S(1)} %bitcast.85) | data formatting | bytes 4718592 | tf_op jit(solution)/shard_map/reshape | solution.py:251
  169.7 10.9 %all-to-all-start.5 = ((bf16[64,2,12,768]{3,1,2,0:T(2,128)(2,1)}), bf16[64,2,12,768]{3,1,2,0:T(2,128)(2,1)}, u32[]{:S(2)}, u32[]{:S(2)}) async-start(bf16[64,2,12,768]{3,1,2,0:T(2,128)(2,1)} %copy.75), calls=%async_computation.5 | async-start | bytes 4718592 | tf_op jit(solution)/shard_map/all_to_all | solution.py:22
  183.5 5.4 %fusion = bf16[1,256,1536]{2,1,0:T(8,128)(2,1)} fusion(bf16[1536,1536]{1,0:T(8,128)(2,1)} %param.23, bf16[1536,768]{1,0:T(8,128)(2,1)S(1)} %copy-done, bf16[32,8,768]{2,1,0:T(8,128)(2,1)} %all-to-all-done.4), kind=kOutput, calls=%fused_computation.4 | convolution fusion | flops 1812725760 | bytes 8257536 | tf_op jit(solution)/shard_map/se,fe->sf/dot_general | solution.py:257
  188.9 2.1 convert_reduce_fusion.1
  191.0 21.4 %all-to-all-done.5 = bf16[64,2,12,768]{3,1,2,0:T(2,128)(2,1)} async-done(((bf16[64,2,12,768]{3,1,2,0:T(2,128)(2,1)}), bf16[64,2,12,768]{3,1,2,0:T(2,128)(2,1)}, u32[]{:S(2)}, u32[]{:S(2)}) %all-to-all-start.5) | async-done | bytes 2359328 | tf_op jit(solution)/shard_map/all_to_all | solution.py:22
  212.4 3.6 %convert_reduce_fusion = f32[2,12,768]{2,0,1:T(2,128)S(1)} fusion(bf16[64,2,12,768]{3,1,2,0:T(2,128)(2,1)} %all-to-all-done.5), kind=kLoop, calls=%fused_computation | loop fusion | flops 2340864 | bytes 2433024 | tf_op jit(solution)/shard_map/reduce_sum | solution.py:252
  216.0 5.2 %all_to_all.57 = f32[2,12,768]{2,1,0:T(8,128)S(1)} all-to-all(f32[2,12,768]{2,1,0:T(8,128)S(1)} %copy.76), channel_id=1, replica_groups=mesh['zh'=2,'co'=2,'y'=4,'x'=4,'zl'=2] {'co'}, dimensions={0} | all-to-all | bytes 147456 | tf_op jit(solution)/shard_map/all_to_all | solution.py:22
  221.9 2.6 %fusion.17 = f32[12,1536]{1,0:T(8,128)} fusion(bf16[1536,768]{1,0:T(8,128)(2,1)S(1)} %copy-done, f32[2,12,768]{2,1,0:T(8,128)S(1)} %all_to_all.57), kind=kOutput, calls=%fused_computation.41 | convolution fusion | flops 169869312 | bytes 2482176 | tf_op jit(solution)/shard_map/dot_general | solution.py:260
  (58 shorter events, 19.9 us)
Async XLA Ops:
  0.6 182.9 %copy-start = (bf16[1536,768]{1,0:T(8,128)(2,1)S(1)}, bf16[1536,768]{1,0:T(8,128)(2,1)}, u32[]{:S(2)}) copy-start(bf16[1536,768]{1,0:T(8,128)(2,1)} %param.22) | copy-start | bytes 7077892
  3.6 19.2 %copy-start.7 = (s32[8]{0:T(128)S(1)}, s32[8]{0:T(128)}, u32[]{:S(2)}) copy-start(s32[8]{0:T(128)} %param.18) | copy-start | bytes 100
  3.6 20.4 %copy-start.8 = (s32[8]{0:T(128)S(1)}, s32[8]{0:T(128)}, u32[]{:S(2)}) copy-start(s32[8]{0:T(128)} %param.17) | copy-start | bytes 100
  18.7 13.8 %all-to-all-start.1 = ((bf16[4,8,96,128]{3,2,1,0:T(8,128)(2,1)}), bf16[4,8,96,128]{3,2,1,0:T(8,128)(2,1)S(1)}, u32[]{:S(2)}, u32[]{:S(2)}) async-start(bf16[4,8,96,128]{3,2,1,0:T(8,128)(2,1)} %broadcast_in_dim.8), calls=%async_computation.1 | async-start | bytes 1572864 | tf_op jit(solution)/shard_map/all_to_all | solution.py:22
  32.5 0.9 copy-start.4
  33.4 33.2 %copy-start.6 = (bf16[1,128,768]{2,1,0:T(8,128)(2,1)S(1)}, bf16[1,128,768]{2,1,0:T(8,128)(2,1)}, u32[]{:S(2)}) copy-start(bf16[1,128,768]{2,1,0:T(8,128)(2,1)} %param.12) | copy-start | bytes 589828
  66.5 5.7 %copy-start.9 = (s32[1,128,1]{1,2,0:T(1,128)S(1)}, s32[1,128,1]{1,2,0:T(1,128)}, u32[]{:S(2)}) copy-start(s32[1,128,1]{1,2,0:T(1,128)} %param.19) | copy-start | bytes 1540
  67.8 4.8 %copy-start.5 = (bf16[8,96,128]{2,1,0:T(8,128)(2,1)S(1)}, bf16[8,96,128]{2,1,0:T(8,128)(2,1)}, u32[]{:S(2)}) copy-start(bf16[8,96,128]{2,1,0:T(8,128)(2,1)} %get-tuple-element.7) | copy-start | bytes 589828
  67.8 23.7 %all-to-all-start.7 = ((bf16[8,128,768]{2,1,0:T(8,128)(2,1)}), bf16[8,128,768]{2,1,0:T(8,128)(2,1)}, u32[]{:S(2)}, u32[]{:S(2)}) async-start(bf16[8,128,768]{2,1,0:T(8,128)(2,1)} %broadcast_in_dim.11), calls=%async_computation.7 | async-start | bytes 3145728 | tf_op jit(solution)/shard_map/all_to_all | solution.py:22
  91.5 10.8 %all-to-all-start.3 = ((bf16[8,192,128]{2,1,0:T(8,128)(2,1)}), bf16[8,192,128]{2,1,0:T(8,128)(2,1)S(1)}, u32[]{:S(2)}, u32[]{:S(2)}) async-start(bf16[8,192,128]{2,1,0:T(8,128)(2,1)} %pad_maximum_fusion.1), calls=%async_computation.3 | async-start | bytes 786432 | tf_op jit(solution)/shard_map/all_to_all | solution.py:22
  96.0 17.8 %copy-start.2 = (bf16[1,128,768]{2,1,0:T(8,128)(2,1)S(1)}, bf16[1,128,768]{2,1,0:T(8,128)(2,1)}, u32[]{:S(2)}) copy-start(bf16[1,128,768]{2,1,0:T(8,128)(2,1)} %param.14) | copy-start | bytes 589828
  102.3 9.6 %copy-start.3 = (bf16[8,192,128]{2,1,0:T(8,128)(2,1)}, bf16[8,192,128]{2,1,0:T(8,128)(2,1)S(1)}, u32[]{:S(2)}) copy-start(bf16[8,192,128]{2,1,0:T(8,128)(2,1)S(1)} %all-to-all-done.3) | copy-start | bytes 1179652
  102.3 19.3 %all-to-all-start.8 = ((bf16[16,48,144]{2,1,0:T(8,128)(2,1)}), bf16[16,48,144]{2,1,0:T(8,128)(2,1)}, u32[]{:S(2)}, u32[]{:S(2)}) async-start(bf16[16,48,144]{2,1,0:T(8,128)(2,1)} %bitcast.30), calls=%async_computation.8 | async-start | bytes 786432 | tf_op jit(solution)/shard_map/all_to_all | solution.py:22
  112.0 14.3 %copy-start.1 = (bf16[1,256,1536]{2,1,0:T(8,128)(2,1)S(1)}, bf16[1,256,1536]{2,1,0:T(8,128)(2,1)}, u32[]{:S(2)}) copy-start(bf16[1,256,1536]{2,1,0:T(8,128)(2,1)} %param.21) | copy-start | bytes 2359300
  121.6 14.2 %all-to-all-start.4 = ((bf16[32,8,768]{2,1,0:T(8,128)(2,1)}), bf16[32,8,768]{2,1,0:T(8,128)(2,1)}, u32[]{:S(2)}, u32[]{:S(2)}) async-start(bf16[32,8,768]{2,1,0:T(8,128)(2,1)} %fusion.1), calls=%async_computation.4 | async-start | bytes 786432 | tf_op jit(solution)/shard_map/all_to_all | solution.py:22
  127.2 27.7 %collective-permute-start = (bf16[256,1536]{1,0:T(8,128)(2,1)}, bf16[256,1536]{1,0:T(8,128)(2,1)}, u32[]{:S(2)}, u32[]{:S(2)}) collective-permute-start(bf16[256,1536]{1,0:T(8,128)(2,1)} %select_bitcast_fusion), channel_id=1, source_target_pairs={{0,32},{32,0},{1,33},{33,1},{2,34},{34,2},{3,35},{35,3},{4,36},{36... | collective-permute-start | bytes 2359304 | tf_op jit(solution)/shard_map/ppermute | solution.py:201
  135.8 9.3 %all-to-all-start.9 = ((f32[8,1,864]{2,1,0:T(1,128)}), f32[8,1,864]{2,1,0:T(1,128)}, u32[]{:S(2)}, u32[]{:S(2)}) async-start(f32[8,1,864]{2,1,0:T(1,128)} %reshape.99), calls=%async_computation.9 | async-start | bytes 57344 | tf_op jit(solution)/shard_map/all_to_all | solution.py:22
  142.9 12.0 %collective-permute-start.1 = (bf16[256,768]{1,0:T(8,128)(2,1)}, bf16[256,768]{1,0:T(8,128)(2,1)S(1)}, u32[]{:S(2)}, u32[]{:S(2)}) collective-permute-start(bf16[256,768]{1,0:T(8,128)(2,1)} %bitcast.18), channel_id=1, source_target_pairs={{0,32},{32,0},{1,33},{33,1},{2,34},{34,2},{3,35},{35,3},{4,36},{36... | collective-permute-start | bytes 1179656 | tf_op jit(solution)/shard_map/ppermute | solution.py:244
  145.1 24.6 %all-to-all-start.10 = ((bf16[128,3,768]{2,1,0:T(4,128)(2,1)}), bf16[128,3,768]{2,1,0:T(4,128)(2,1)}, u32[]{:S(2)}, u32[]{:S(2)}) async-start(bf16[128,3,768]{2,1,0:T(4,128)(2,1)} %reshape.97), calls=%async_computation.10 | async-start | bytes 1572864 | tf_op jit(solution)/shard_map/all_to_all | solution.py:22
  169.7 42.7 %all-to-all-start.5 = ((bf16[64,2,12,768]{3,1,2,0:T(2,128)(2,1)}), bf16[64,2,12,768]{3,1,2,0:T(2,128)(2,1)}, u32[]{:S(2)}, u32[]{:S(2)}) async-start(bf16[64,2,12,768]{3,1,2,0:T(2,128)(2,1)} %copy.75), calls=%async_computation.5 | async-start | bytes 4718592 | tf_op jit(solution)/shard_map/all_to_all | solution.py:22

commit v2 on v1

v2 whole, which is shorter than its diff:
```python
from functools import partial

import jax
import jax.numpy as jnp
from jax import lax
from jax.experimental import pallas as pl
from jax.experimental.pallas import tpu as pltpu
from jax.sharding import Mesh, PartitionSpec as P

F32 = jnp.float32
BF16 = jnp.bfloat16
DP = ("zh", "co")
SEQ = ("y", "x", "zl")
GRP = ("x", "zl")
ALL = DP + SEQ
QB = 256
KC = 512
LOG2E = 1.4426950408889634


def exchange(x, axes):
    return lax.all_to_all(x, axes, 0, 0, tiled=True)


def sent_to_all(x, axes):
    n = lax.axis_size(axes)
    return exchange(jnp.broadcast_to(x[None], (n, *x.shape)), axes)


def blocks_turned(srcs, lane, sub, count):
    outs = []
    for a in range(count):
        out = None
        for b in range(count):
            shift = (b - a) % count * sub
            moved = pltpu.roll(srcs[b], shift, 1) if shift else srcs[b]
            out = moved if out is None else jnp.where(lane == b, moved, out)
        outs.append(out)
    return outs


def attention_kernel(
    par, mine, back, kmat, vmat, kt, vt, code, score, prob, dk, dv, *, hd, tok, nkb, ny, scaling
):
    step = pl.program_id(0)
    length = nkb * tok
    sub = tok // ny
    part = 2 * hd // ny
    off = par[0]
    inv_len, dil, inv_dil = par[1], par[2], par[3]

    def code_of(pos):
        seg = jnp.floor((pos + 0.5) * inv_len)
        res = pos - dil * jnp.floor((pos + 0.5) * inv_dil)
        return seg * 8.0 + res

    @pl.when(step == 0)
    def _():
        for b in range(nkb):
            kb = mine[b, :hd, :]
            vb = mine[b, hd : 2 * hd, :]
            kt[:, b * tok : (b + 1) * tok] = kb
            vt[:, b * tok : (b + 1) * tok] = vb
            kmat[b * tok : (b + 1) * tok, :] = kb.astype(F32).T.astype(BF16)
            vmat[b * tok : (b + 1) * tok, :] = vb.astype(F32).T.astype(BF16)
            pos = lax.broadcasted_iota(jnp.int32, (tok, 128), 0).astype(F32) + float(b * tok)
            code[b * tok : (b + 1) * tok, :] = code_of(pos)
        dk[...] = jnp.zeros_like(dk)
        dv[...] = jnp.zeros_like(dv)

    nb = QB // sub
    lane = lax.broadcasted_iota(jnp.int32, (part, tok), 1) // sub
    tiles = []
    for first in range(0, nb, ny):
        srcs = [mine[step * nb + first + y, 2 * hd :, :].astype(F32) for y in range(ny)]
        tiles.append(jnp.concatenate(blocks_turned(srcs, lane, sub, ny), axis=0))
    qd = jnp.concatenate(tiles, axis=1)
    qt = qd[:hd, :].astype(BF16)
    dot_ = qd[hd:, :]
    qidx = lax.broadcasted_iota(jnp.int32, (8, QB), 1).astype(F32) + (step * QB).astype(F32)
    qpos = qidx + float(tok - sub) * jnp.floor(qidx * (1.0 / sub)) + off
    qcode = code_of(qpos)[0:1, :]

    mx = jnp.full((8, QB), -3e38, F32)
    for c in range(length // KC):
        rows = slice(c * KC, (c + 1) * KC)
        s = jnp.dot(kmat[rows, :], qt, preferred_element_type=F32)
        ck = code[rows, :]
        s = jnp.where(jnp.concatenate([ck] * (QB // 128), axis=1) == qcode, s, -1e30)
        score[rows, :] = s
        mx = jnp.maximum(mx, jnp.max(s.reshape(KC // 8, 8, QB), axis=0))
    top = jnp.max(mx, axis=0, keepdims=True)

    tot = jnp.zeros((8, QB), F32)
    ot = jnp.zeros((hd, QB), F32)
    for c in range(length // KC):
        rows = slice(c * KC, (c + 1) * KC)
        p = jnp.exp2((score[rows, :] - top) * (scaling * LOG2E))
        tot = tot + jnp.sum(p.reshape(KC // 8, 8, QB), axis=0)
        ph = p.astype(BF16)
        prob[rows, :] = ph
        ot = ot + jnp.dot(vt[:, rows], ph, preferred_element_type=F32)
    inv = 1.0 / jnp.sum(tot, axis=0, keepdims=True)
    ot = ot * inv
    dn = dot_ * inv
    dnh = dn.astype(BF16)
    delta = jnp.sum(dnh.astype(F32) * ot, axis=0, keepdims=True)
    dmat = dn.T.astype(BF16)
    qmat = qt.astype(F32).T.astype(BF16)

    dqt = jnp.zeros((hd, QB), F32)
    for c in range(length // KC):
        rows = slice(c * KC, (c + 1) * KC)
        ph = prob[rows, :]
        dp = jnp.dot(vmat[rows, :], dnh, preferred_element_type=F32)
        ds = (ph.astype(F32) * (dp - delta)).astype(BF16)
        dv[rows, :] += jnp.dot(ph, dmat, preferred_element_type=F32)
        dk[rows, :] += jnp.dot(ds, qmat, preferred_element_type=F32)
        dqt = dqt + jnp.dot(kt[:, rows], ds, preferred_element_type=F32)

    both = jnp.concatenate([dqt * scaling, ot], axis=0)
    for first in range(0, nb, ny):
        cols = slice(first * sub, (first + ny) * sub)
        srcs = [both[g * part : (g + 1) * part, cols] for g in range(ny)]
        for y, block in enumerate(blocks_turned(srcs, lane, sub, ny)):
            back[step * nb + first + y, 2 * hd :, :] = block.astype(BF16)

    @pl.when(step == pl.num_programs(0) - 1)
    def _():
        for b in range(nkb):
            rows = slice(b * tok, (b + 1) * tok)
            back[b, :hd, :] = (dk[rows, :].T * scaling).astype(BF16)
            back[b, hd : 2 * hd, :] = dv[rows, :].T.astype(BF16)


def attention_grads(par, mine, hd, ny, scaling):
    nkb, rows, tok = mine.shape
    length = nkb * tok
    steps = length // ny // QB
    whole = pl.BlockSpec((nkb, rows, tok), lambda i: (0, 0, 0))
    return pl.pallas_call(
        partial(attention_kernel, hd=hd, tok=tok, nkb=nkb, ny=ny, scaling=scaling),
        grid=(steps,),
        out_shape=jax.ShapeDtypeStruct((nkb, rows, tok), BF16),
        in_specs=[pl.BlockSpec(memory_space=pltpu.SMEM), whole],
        out_specs=whole,
        scratch_shapes=[
            pltpu.VMEM((length, hd), BF16),
            pltpu.VMEM((length, hd), BF16),
            pltpu.VMEM((hd, length), BF16),
            pltpu.VMEM((hd, length), BF16),
            pltpu.VMEM((length, 128), F32),
            pltpu.VMEM((length, QB), F32),
            pltpu.VMEM((length, QB), BF16),
            pltpu.VMEM((length, hd), F32),
            pltpu.VMEM((length, hd), F32),
        ],
        compiler_params=pltpu.CompilerParams(dimension_semantics=("arbitrary",)),
        cost_estimate=pl.CostEstimate(
            flops=30_000_000_000, bytes_accessed=4_000_000, transcendentals=length * length // ny
        ),
        name="attention_grads",
    )(par, mine)


def pack_kernel(saved, cot, weight, out, *, heads, hd, tok, ny):
    sub = tok // ny
    part = 2 * hd // ny
    width = heads * hd
    grads = lax.dot_general(
        weight[...], cot[...], (((1,), (1,)), ((), ())), preferred_element_type=F32
    )
    grads = grads.astype(BF16).astype(F32)
    saved_t = saved[...].astype(F32).T
    lane = lax.broadcasted_iota(jnp.int32, (part, tok), 1) // sub
    for h in range(heads):
        rows = slice(h * hd, (h + 1) * hd)
        keys = saved_t[width + h * hd : width + (h + 1) * hd, :].astype(BF16)
        values = saved_t[2 * width + h * hd : 2 * width + (h + 1) * hd, :].astype(BF16)
        both = jnp.concatenate([saved_t[rows, :], grads[rows, :]], axis=0)
        srcs = [both[g * part : (g + 1) * part, :] for g in range(ny)]
        for y, block in enumerate(blocks_turned(srcs, lane, sub, ny)):
            out[y * heads + h, :hd, :] = keys
            out[y * heads + h, hd : 2 * hd, :] = values
            out[y * heads + h, 2 * hd :, :] = block.astype(BF16)


def packed(saved, cot, weight, heads, ny):
    tok = saved.shape[0]
    hd = weight.shape[0] // heads
    rows = 2 * hd + 2 * hd // ny
    return pl.pallas_call(
        partial(pack_kernel, heads=heads, hd=hd, tok=tok, ny=ny),
        out_shape=jax.ShapeDtypeStruct((ny * heads, rows, tok), BF16),
        cost_estimate=pl.CostEstimate(
            flops=2 * weight.size * tok, bytes_accessed=2_000_000, transcendentals=0
        ),
        name="packed",
    )(saved, cot, weight)


def unpack_kernel(got, grads, attention, *, heads, hd, tok, ny):
    sub = tok // ny
    part = 2 * hd // ny
    width = heads * hd
    lane = lax.broadcasted_iota(jnp.int32, (part, tok), 1) // sub
    for h in range(heads):
        total = got[h, : 2 * hd, :].astype(F32)
        for y in range(1, ny):
            total = total + got[y * heads + h, : 2 * hd, :].astype(F32)
        total = total.astype(BF16)
        grads[width + h * hd : width + (h + 1) * hd, :] = total[:hd, :]
        grads[2 * width + h * hd : 2 * width + (h + 1) * hd, :] = total[hd:, :]
        srcs = [got[y * heads + h, 2 * hd :, :].astype(F32) for y in range(ny)]
        both = jnp.concatenate(blocks_turned(srcs, lane, sub, ny), axis=0)
        grads[h * hd : (h + 1) * hd, :] = both[:hd, :].astype(BF16)
        attention[h * hd : (h + 1) * hd, :] = both[hd:, :].astype(BF16)


def unpacked(got, heads, hd, ny):
    tok = got.shape[2]
    return pl.pallas_call(
        partial(unpack_kernel, heads=heads, hd=hd, tok=tok, ny=ny),
        out_shape=(
            jax.ShapeDtypeStruct((3 * heads * hd, tok), BF16),
            jax.ShapeDtypeStruct((heads * hd, tok), BF16),
        ),
        cost_estimate=pl.CostEstimate(
            flops=got.size * 100, bytes_accessed=2_000_000, transcendentals=0
        ),
        name="unpacked",
    )(got)


def summed_kernel(keep, other, incoming, swapped, small, out):
    d_slide = incoming.shape[1]
    total = jnp.dot(keep[...], incoming[...], preferred_element_type=F32)
    total = total + jnp.dot(other[...], swapped[...], preferred_element_type=F32)
    out[:, :d_slide] = total.astype(BF16)
    out[:, d_slide:] = small[...]


def summed_terms(keep, other, incoming, swapped, small):
    rows, slots = keep.shape
    d_slide = incoming.shape[1]
    block = 512
    wide = d_slide + small.shape[1]
    whole = pl.BlockSpec((slots, d_slide), lambda i: (0, 0))
    return pl.pallas_call(
        summed_kernel,
        grid=(rows // block,),
        out_shape=jax.ShapeDtypeStruct((rows, wide), BF16),
        in_specs=[
            pl.BlockSpec((block, slots), lambda i: (i, 0)),
            pl.BlockSpec((block, slots), lambda i: (i, 0)),
            whole,
            whole,
            pl.BlockSpec((block, small.shape[1]), lambda i: (i, 0)),
        ],
        out_specs=pl.BlockSpec((block, wide), lambda i: (i, 0)),
        compiler_params=pltpu.CompilerParams(dimension_semantics=("arbitrary",)),
        cost_estimate=pl.CostEstimate(
            flops=4 * rows * slots * d_slide, bytes_accessed=8_000_000, transcendentals=0
        ),
        name="summed_terms",
    )(keep, other, incoming, swapped, small)


def one_hot_rows(source, width, keep=None):
    hit = source[:, None] == jnp.arange(width, dtype=jnp.int32)[None, :]
    if keep is not None:
        hit = hit & keep[:, None]
    return hit.astype(BF16)


def picked_rows(onehot, x):
    return jnp.einsum("rx,tx->rt", onehot, x, preferred_element_type=F32).astype(BF16)


def local(
    tile_embed,
    qkv_saved,
    out_cotangent,
    qkv_weight,
    out_weight,
    seg_length,
    dilation,
    owner_map,
    tile_hidden,
    tile_output,
    embed_weight,
    proj_weight,
):
    heads = seg_length.shape[0]
    width = out_weight.shape[0]
    hd = width // heads
    tok = qkv_saved.shape[1]
    d_slide = tile_embed.shape[2]
    n_seq = lax.axis_size(SEQ)
    n_y = lax.axis_size("y")
    n_dp = lax.axis_size(DP)
    n_dev = n_dp * n_seq
    scaling = hd ** (-0.5)
    cot = out_cotangent[0]
    head = lax.axis_index(GRP)
    core = lax.axis_index("co")

    outgoing = packed(qkv_saved[0], cot, out_weight, heads, n_y)
    outgoing, hidden_rows, output_rows = lax.optimization_barrier(
        (outgoing, tile_hidden[0], tile_output[0])
    )
    mine = exchange(outgoing, SEQ)

    seg = seg_length[head].astype(F32)
    dil = dilation[head].astype(F32)
    off = (lax.axis_index("y") * (tok // n_y)).astype(F32)
    par = jnp.stack([off, 1.0 / seg, dil, 1.0 / dil])
    back = attention_grads(par, mine, hd, n_y, scaling)

    swap = partial(lax.ppermute, axis_name="co", perm=[(0, 1), (1, 0)])
    low = core == 0
    d_tile = embed_weight.shape[0]
    holders = n_dev // 2
    per = d_tile // n_dev
    half = per // 2
    row = jnp.arange(d_tile, dtype=jnp.int32)
    holder = row // (2 * per)
    to_core = row // per % 2
    owner = (holder // n_seq * 2 + to_core) * n_seq + holder % n_seq
    second = row // half % 2 == 1
    spot = row % half
    tile_rows = one_hot_rows(owner * per + row % per, d_tile)
    keep = picked_rows(tile_rows, jnp.where(low, output_rows, hidden_rows))
    other = swap(picked_rows(tile_rows, jnp.where(low, hidden_rows, output_rows)))
    embed_rows = tile_embed[0]
    embed_pair = jnp.concatenate([embed_rows, swap(embed_rows)], axis=0)
    cot_pair = jnp.concatenate([cot, swap(cot)], axis=0)
    first_rows = picked_rows(one_hot_rows(owner * half + spot, d_slide, ~second), embed_pair)
    second_rows = picked_rows(one_hot_rows(owner * half + spot, d_slide, second), embed_pair)
    back, first_rows, second_rows, cot_pair = lax.optimization_barrier(
        (back, first_rows, second_rows, cot_pair)
    )
    got, keep, other = lax.optimization_barrier((exchange(back, SEQ), keep, other))
    qkv_grad_t, attention_t = unpacked(got, heads, hd, n_y)
    query_key, value_t = qkv_grad_t[: 2 * width], qkv_grad_t[2 * width :]
    embed_grad = (
        cot.astype(F32)
        + jnp.einsum("ct,dc->td", qkv_grad_t, qkv_weight, preferred_element_type=F32)
    ).astype(BF16)

    destination = owner_map[0, :, 0]
    capacity = tile_hidden.shape[1] // n_seq
    onehot = (destination[:, None] == jnp.arange(n_seq, dtype=jnp.int32)[None, :]).astype(F32)
    lower = (
        jnp.arange(tok, dtype=jnp.int32)[:, None] > jnp.arange(tok, dtype=jnp.int32)[None, :]
    ).astype(BF16)
    before = jnp.dot(lower, onehot.astype(BF16), preferred_element_type=F32)
    rank = jnp.sum(before * onehot, axis=1).astype(jnp.int32)
    slot_index = destination * capacity + rank
    selector = (
        jnp.arange(n_seq * capacity, dtype=jnp.int32)[:, None] == slot_index[None, :]
    ).astype(BF16)
    routed = jnp.dot(selector, embed_grad, preferred_element_type=F32).astype(BF16)
    value_att = jnp.concatenate([value_t, attention_t], axis=0)
    routed, query_key, value_att = lax.optimization_barrier((routed, query_key, value_att))
    incoming = exchange(routed.reshape(n_seq, capacity, d_slide), SEQ).reshape(-1, d_slide)
    grads = jnp.where(low, query_key, value_att)
    grads = jnp.concatenate([grads, swap(jnp.where(low, value_att, query_key))], axis=1)
    grads = grads.reshape(2, width, 2 * tok)
    o_half = half // 2
    att_row = owner * o_half + spot % o_half
    att_low = jnp.einsum(
        "ra,at->rt",
        one_hot_rows(att_row, width, second & (spot < o_half)),
        grads[1],
        preferred_element_type=F32,
    ).astype(BF16)
    att_high = jnp.einsum(
        "ra,at->rt",
        one_hot_rows(att_row, width, second & (spot >= o_half)),
        grads[1],
        preferred_element_type=F32,
    ).astype(BF16)
    left_side = jnp.concatenate(
        [first_rows, jnp.where(low, second_rows, att_low), jnp.where(low, 0, att_high)], axis=1
    )
    flat = grads.transpose(0, 2, 1)
    right_side = jnp.concatenate(
        [flat[0], jnp.where(low, flat[1], cot_pair[:, :width]), cot_pair[:, width:]], axis=0
    )
    small = jnp.dot(left_side, right_side, preferred_element_type=F32).astype(BF16)
    incoming, small = lax.optimization_barrier((incoming, small))

    term = summed_terms(keep, other, incoming, swap(incoming), small)
    term = term.reshape(holders, -1, term.shape[1])
    held = jnp.sum(exchange(term, ("zh",) + SEQ).astype(F32), axis=0)
    tile_grad = jnp.einsum("sd,ed->se", incoming, embed_weight, preferred_element_type=F32)
    hidden_grad = jnp.einsum(
        "se,fe->sf", tile_grad.astype(BF16), proj_weight, preferred_element_type=F32
    ).astype(BF16)[None]
    held, hidden_grad = lax.optimization_barrier((held, hidden_grad))
    mine_held = jnp.where(low, held[:per], held[per:])
    pair_held = swap(jnp.where(low, held[per:], held[:per]))
    from_low = jnp.where(low, mine_held, pair_held)
    from_high = jnp.where(low, pair_held, mine_held)
    embed_sum = from_low[:, :d_slide]
    factor = from_high[:, :d_slide]
    q_k, v_o = from_low[:, d_slide:], from_high[:, d_slide:]
    qkv_sum = jnp.concatenate([q_k[:half], q_k[half:], v_o[:half]], axis=1)
    out_sum = jnp.concatenate([v_o[half : half + o_half], v_o[half + o_half :]], axis=1)

    proj_sum = jnp.dot(factor, embed_weight.astype(F32).T, precision=lax.Precision.HIGHEST)
    return (hidden_grad, proj_sum, embed_sum, qkv_sum, out_sum)


def solution(mesh):
    fine = Mesh(mesh.devices.reshape(2, 2, 4, 4, 2), ALL)
    part = P(DP, SEQ, None)
    rows = P(ALL, None)
    return jax.shard_map(
        local,
        mesh=fine,
        in_specs=(part, part, part, P(), P(), P(), P(), part, part, part, P(), P()),
        out_specs=(part, rows, rows, rows, rows),
        check_vma=False,
    )
```

time: 226 us -> 172 us (0.76)
  blocking collectives: 30.4 us -> 0 us
  starting transfers between devices: 54.4 us -> 33.2 us
  local copies, waits for them, and re-layouts: 24.8 us -> 8.24 us
  Pallas kernels: 21.2 us -> 32.2 us
  matrix products: 21.3 us -> 29.7 us
  other arithmetic: 11.5 us -> 8.78 us
    all_to_all x3 -> x0, blocking collectives: 30.4 us -> none  [exchange(): return lax.all_to_all(x, axes, 0, 0, tiled=True)]
    all_to_all x8 -> x4, starting transfers between devices: 49.9 us -> 24.5 us  [exchange(): return lax.all_to_all(x, axes, 0, 0, tiled=True)]
    pallas_call x1 -> x4, Pallas kernels: 21.2 us -> 32.2 us  [the longest x1 21.9 us: attention_grads(): pl.pallas_call(partial(attention_kernel, hd=hd, tok=tok, nkb=nkb, ny=ny,...]
    reshape x6 -> x1, local copies, waits for them, and re-layouts: 11.6 us -> 1.21 us  [local(): grads = grads.reshape(2, width, 2 * tok)]
    dot_general x5 -> x7, matrix products: 9.96 us -> 18.4 us  [the longest x4 12.4 us: picked_rows(): jnp.einsum('rx,tx->rt', onehot, x, preferred_element_type=F32).astype(BF16)]
    reduce_sum x4 -> x1, other arithmetic: 6.88 us -> 2.51 us  [local(): held = jnp.sum(exchange(term, ('zh',) + SEQ).astype(F32), axis=0)]
    ppermute x2 -> x6, starting transfers between devices: 4.51 us -> 8.73 us  [the longest x1 2.71 us: local(): swap(jnp.where(low, value_att, query_key))]
    all_to_all x8 -> x4, waiting for transfers between devices: 58.5 us -> 54.3 us  [exchange(): return lax.all_to_all(x, axes, 0, 0, tiled=True)]
  transfers between devices with their start and end apart: 10 -> 10, of which waited for: 6 -> 6; matrix products, arithmetic and copies ran while one was open for 20% -> 18% of each run, Pallas kernels for 0% -> 2%
where the time goes in v2:
time: 172 us; the launch traced here: 171 us
  waiting for transfers between devices  56.6 us (33%)
  starting transfers between devices  33.2 us (19%)
  Pallas kernels  32.2 us (19%)
  matrix products  29.7 us (17%)
  other arithmetic  8.78 us (5%)
  local copies, waits for them, and re-layouts  8.24 us (5%)
  between operations  2.4 us (1%)
    all_to_all x4, waiting for transfers between devices, exchange(): return lax.all_to_all(x, axes, 0, 0, tiled=True)  54.3 us
    all_to_all x4, starting transfers between devices, exchange(): return lax.all_to_all(x, axes, 0, 0, tiled=True)  24.5 us
    pallas_call x1, Pallas kernels, attention_grads(): pl.pallas_call(partial(attention_kernel, hd=hd, tok=tok, nkb=nkb, ny=ny,...  21.9 us
    dot_general x4, matrix products, picked_rows(): jnp.einsum('rx,tx->rt', onehot, x, preferred_element_type=F32).astype(BF16)  12.4 us
    pallas_call x1, Pallas kernels, summed_terms(): pl.pallas_call(summed_kernel, grid=(rows // block,), out_shape=jax.ShapeD...  5.45 us
    dot_general x1, matrix products, local(): jnp.einsum('se,fe->sf', tile_grad.astype(BF16), proj_weight, preferred_el...  5.25 us
  transfers between devices with their start and end apart: 10, of which 6 were waited for; matrix products, arithmetic and copies ran while one was open for 18% of the time, Pallas kernels for 2%

profile of v2, /device:TPU:1, one launch (start us, length us, event | category | flops | bytes accessed | tf_op | source)
XLA Modules:
  0.0 171.2 jit_solution(9556179472266445597)
XLA Ops:
  0.7 1.5 collective-permute-start
  2.2 2.6 %packed.1 = bf16[32,120,128]{2,1,0:T(8,128)(2,1)} custom-call(bf16[128,1152]{1,0:T(8,128)(2,1)} %bitcast.42, bf16[128,768]{1,0:T(8,128)(2,1)} %bitcast.33, bf16[384,768]{1,0:T(8,128)(2,1)} %weight.1), custom_call_target="tpu_custom_call" | custom-call | flops 75497472 | bytes 2000000 | tf_op jit(solution)/shard_map/packed/pallas_call | solution.py:192
  4.8 8.5 %all-to-all-start = ((bf16[32,120,128]{2,1,0:T(8,128)(2,1)}), bf16[32,120,128]{2,1,0:T(8,128)(2,1)S(1)}, u32[]{:S(2)}, u32[]{:S(2)}) async-start(bf16[32,120,128]{2,1,0:T(8,128)(2,1)} %packed.1), calls=%async_computation | async-start | bytes 1966080 | tf_op jit(solution)/shard_map/all_to_all | solution.py:22
  14.7 1.2 dynamic_slice.6
  17.3 1.7 pad_maximum_fusion.2
  19.0 3.4 %fusion.12 = bf16[1536,256]{1,0:T(8,128)(2,1)} fusion(s32[1536]{0:T(1024)S(1)} %fusion.77, pred[1536]{0:T(1024)(128)(4,1)S(1)} %fusion.72, bf16[128,768]{1,0:T(8,128)(2,1)} %collective-permute-done, bf16[128,768]{1,0:T(8,128)(2,1)} %bitcast.48), kind=kOutput, calls=%fused_computation.15 | convolution fusion | flops 607518720 | bytes 1187328 | tf_op jit(solution)/shard_map/rx,tx->rt/dot_general | solution.py:277
  22.4 3.2 %fusion.15 = bf16[1536,256]{1,0:T(8,128)(2,1)} fusion(s32[1536]{0:T(1024)S(1)} %fusion.77, pred[1536]{0:T(1024)(128)(4,1)S(1)} %fusion.92, bf16[128,768]{1,0:T(8,128)(2,1)} %collective-permute-done, bf16[128,768]{1,0:T(8,128)(2,1)S(1)} %bitcast.49), kind=kOutput, calls=%fused_computation.16 | convolution fusion | flops 607518720 | bytes 1187328 | tf_op jit(solution)/shard_map/rx,tx->rt/dot_general | solution.py:277
  25.6 3.9 %all-to-all-done.mine = bf16[32,120,128]{2,1,0:T(8,128)(2,1)S(1)} async-done(((bf16[32,120,128]{2,1,0:T(8,128)(2,1)}), bf16[32,120,128]{2,1,0:T(8,128)(2,1)S(1)}, u32[]{:S(2)}, u32[]{:S(2)}) %all-to-all-start) | async-done | bytes 983072 | tf_op jit(solution)/shard_map/all_to_all | solution.py:22
  30.5 21.9 %attention_grads.1 = bf16[32,120,128]{2,1,0:T(8,128)(2,1)} custom-call(f32[4]{0:T(128)} %pad_maximum_fusion.8.par, bf16[32,120,128]{2,1,0:T(8,128)(2,1)} %copy-done.6), custom_call_target="tpu_custom_call" | custom-call | flops 30000001024 | bytes 4000000 | tf_op jit(solution)/shard_map/attention_grads/pallas_call | solution.py:141
  52.4 4.1 %all-to-all-start.1 = ((bf16[32,120,128]{2,1,0:T(8,128)(2,1)}), bf16[32,120,128]{2,1,0:T(8,128)(2,1)S(1)}, u32[]{:S(2)}, u32[]{:S(2)}) async-start(bf16[32,120,128]{2,1,0:T(8,128)(2,1)} %attention_grads.1), calls=%async_computation.1 | async-start | bytes 1966080 | tf_op jit(solution)/shard_map/all_to_all | solution.py:22
  56.6 3.1 %fusion.11 = bf16[1536,256]{1,0:T(8,128)(2,1)S(1)} fusion(s32[1536]{0:T(1024)S(1)} %fusion.80, bf16[256,1536]{1,0:T(8,128)(2,1)} %bitcast.45, bf16[256,1536]{1,0:T(8,128)(2,1)} %bitcast.43, pred[]{:T(512)S(6)} %eq.137), kind=kOutput, calls=%fused_computation.14 | convolution fusion | flops 1211105280 | bytes 2365441 | tf_op jit(solution)/shard_map/rx,tx->rt/dot_general | solution.py:277
  59.7 1.9 %collective-permute-start.2 = (bf16[1536,256]{1,0:T(8,128)(2,1)S(1)}, bf16[1536,256]{1,0:T(8,128)(2,1)}, u32[]{:S(2)}, u32[]{:S(2)}) collective-permute-start(bf16[1536,256]{1,0:T(8,128)(2,1)S(1)} %fusion.11), channel_id=1, source_target_pairs={{0,32},{32,0},{1,33},{33,1},{2,34},{34,2},{3,35},{35,3},{4,36},{36... | collective-permute-start | bytes 2359304 | tf_op jit(solution)/shard_map/ppermute | solution.py:334
  61.8 2.7 %fusion.10.keep = bf16[1536,256]{1,0:T(8,128)(2,1)} fusion(s32[1536]{0:T(1024)S(1)} %fusion.80, bf16[256,1536]{1,0:T(8,128)(2,1)S(1)} %bitcast.44, bf16[256,1536]{1,0:T(8,128)(2,1)S(1)} %bitcast.46, pred[]{:T(512)S(6)} %eq.137), kind=kOutput, calls=%fused_computation.13 | convolution fusion | flops 1211105280 | bytes 2365441 | tf_op jit(solution)/shard_map/rx,tx->rt/dot_general | solution.py:277
  64.6 7.2 %all-to-all-done.1.got = bf16[32,120,128]{2,1,0:T(8,128)(2,1)S(1)} async-done(((bf16[32,120,128]{2,1,0:T(8,128)(2,1)}), bf16[32,120,128]{2,1,0:T(8,128)(2,1)S(1)}, u32[]{:S(2)}, u32[]{:S(2)}) %all-to-all-start.1) | async-done | bytes 983072 | tf_op jit(solution)/shard_map/all_to_all | solution.py:22
  72.7 2.2 %unpacked.1 = (bf16[1152,128]{1,0:T(8,128)(2,1)}, bf16[384,128]{1,0:T(8,128)(2,1)}) custom-call(bf16[32,120,128]{2,1,0:T(8,128)(2,1)} %copy-done.1), custom_call_target="tpu_custom_call" | custom-call | flops 49152000 | bytes 2000000 | tf_op jit(solution)/shard_map/unpacked/pallas_call | solution.py:222
  77.7 3.3 %convolution_convert_fusion.5 = bf16[256,768]{1,0:T(8,128)(2,1)} fusion(bf16[1152,128]{1,0:T(8,128)(2,1)} %get-tuple-element.31, bf16[768,1152]{1,0:T(8,128)(2,1)} %param.15, s32[128]{0:T(128)S(1)} %convert_add_fusion, bf16[1,128,768]{2,1,0:T(8,128)(2,1)S(1)} %copy-done.2), kind=kOutput, calls=%fused_computation.34 | convolution fusion | flops 277348352 | bytes 2654720 | tf_op jit(solution)/shard_map/dot_general | solution.py:363
  81.7 2.7 %collective-permute-start.3 = (bf16[768,128]{1,0:T(8,128)(2,1)}, bf16[768,128]{1,0:T(8,128)(2,1)S(1)}, u32[]{:S(2)}, u32[]{:S(2)}) collective-permute-start(bf16[768,128]{1,0:T(8,128)(2,1)} %get-tuple-element.45), channel_id=1, source_target_pairs={{0,32},{32,0},{1,33},{33,1},{2,34},{34,2},{3,35},{35,3},{4,36},{36... | collective-permute-start | bytes 589832 | tf_op jit(solution)/shard_map/ppermute | solution.py:368
  84.4 3.9 %all-to-all-start.2 = ((bf16[32,8,768]{2,1,0:T(8,128)(2,1)}), bf16[32,8,768]{2,1,0:T(8,128)(2,1)S(1)}, u32[]{:S(2)}, u32[]{:S(2)}) async-start(bf16[32,8,768]{2,1,0:T(8,128)(2,1)} %bitcast.41), calls=%async_computation.2 | async-start | bytes 786432 | tf_op jit(solution)/shard_map/all_to_all | solution.py:22
  89.2 1.2 copy.18
  90.5 2.3 %convolution_convert_fusion.4 = bf16[1536,256]{1,0:T(8,128)(2,1)S(1)} fusion(s32[1536]{0:T(1024)S(1)} %fusion.73, pred[1536]{0:T(1024)(128)(4,1)S(1)} %fusion.88, bf16[768,128]{1,0:T(8,128)(2,1)} %copy-done.8, bf16[768,128]{1,0:T(8,128)(2,1)} %copy-done.11), kind=kOutput, calls=%fused_computation.19 | convolution fusion | flops 303955968 | bytes 1187328 | tf_op jit(solution)/shard_map/ra,at->rt/dot_general | solution.py:372
  92.9 1.3 fusion.18
  94.3 2.4 %convolution_convert_fusion.small = bf16[1536,384]{1,0:T(8,128)(2,1)} fusion(bf16[1536,256]{1,0:T(8,128)(2,1)S(1)} %fusion.18, bf16[1536,256]{1,0:T(8,128)(2,1)S(1)} %broadcast_select_fusion, bf16[1536,256]{1,0:T(8,128)(2,1)S(1)} %copy-done.18, bf16[256,384]{1,0:T(8,128)(2,1)S(1)} %get-tuple-element.44, bf16[256,384]{1,0:T(8,128)(2,1)S(1)} %get-tuple-element.43, ...), kind=kOutput, calls=%fused_computation.11 | convolution fusion | flops 915406848 | bytes 4128768 | tf_op jit(solution)/shard_map/dot_general | solution.py:391
  96.7 2.3 %all-to-all-done.2 = bf16[32,8,768]{2,1,0:T(8,128)(2,1)S(1)} async-done(((bf16[32,8,768]{2,1,0:T(8,128)(2,1)}), bf16[32,8,768]{2,1,0:T(8,128)(2,1)S(1)}, u32[]{:S(2)}, u32[]{:S(2)}) %all-to-all-start.2) | async-done | bytes 393248 | tf_op jit(solution)/shard_map/all_to_all | solution.py:22
  98.9 1.2 collective-permute-start.4
  100.1 1.3 collective-permute-done.4.swapped
  102.2 5.5 %summed_terms.1 = bf16[1536,1152]{1,0:T(8,128)(2,1)} custom-call(bf16[1536,256]{1,0:T(8,128)(2,1)} %fusion.10.keep, bf16[1536,256]{1,0:T(8,128)(2,1)} %collective-permute-done.2.other, bf16[256,768]{1,0:T(8,128)(2,1)} %bitcast.36, bf16[256,768]{1,0:T(8,128)(2,1)} %copy-done.10, bf16[1536,384]{1,0:T(8,128)(2,1)} %convolution_convert_fusion.small), custom_call_target="tpu_custom_call" | custom-call | flops 1207959552 | bytes 8000000 | tf_op jit(solution)/shard_map/summed_terms/pallas_call | solution.py:249
  107.6 8.0 %all-to-all-start.3 = ((bf16[64,24,1152]{2,1,0:T(8,128)(2,1)}), bf16[64,24,1152]{2,1,0:T(8,128)(2,1)}, u32[]{:S(2)}, u32[]{:S(2)}) async-start(bf16[64,24,1152]{2,1,0:T(8,128)(2,1)} %bitcast.31), calls=%async_computation.3 | async-start | bytes 7077888 | tf_op jit(solution)/shard_map/all_to_all | solution.py:22
  115.7 5.3 %fusion.19 = bf16[1,256,1536]{2,1,0:T(8,128)(2,1)} fusion(bf16[1536,1536]{1,0:T(8,128)(2,1)} %param.23, bf16[256,768]{1,0:T(8,128)(2,1)S(1)} %bitcast.37, bf16[1536,768]{1,0:T(8,128)(2,1)S(1)} %copy-done), kind=kOutput, calls=%fused_computation.21 | convolution fusion | flops 1812725760 | bytes 8257536 | tf_op jit(solution)/shard_map/se,fe->sf/dot_general | solution.py:398
  120.9 41.0 %all-to-all-done.3 = bf16[64,24,1152]{2,1,0:T(8,128)(2,1)} async-done(((bf16[64,24,1152]{2,1,0:T(8,128)(2,1)}), bf16[64,24,1152]{2,1,0:T(8,128)(2,1)}, u32[]{:S(2)}, u32[]{:S(2)}) %all-to-all-start.3) | async-done | bytes 3538976 | tf_op jit(solution)/shard_map/all_to_all | solution.py:22
  161.9 2.5 %convert_reduce_fusion = f32[24,1152]{1,0:T(8,128)S(1)} fusion(bf16[64,24,1152]{2,1,0:T(8,128)(2,1)} %all-to-all-done.3), kind=kLoop, calls=%fused_computation.3 | loop fusion | flops 3511296 | bytes 3649536 | tf_op jit(solution)/shard_map/reduce_sum | solution.py:396
  164.5 1.4 collective-permute-start.5
  166.8 2.6 %fusion.52 = f32[12,1536]{1,0:T(8,128)} fusion(bf16[1536,768]{1,0:T(8,128)(2,1)S(1)} %copy-done, f32[12,1152]{1,0:T(8,128)S(1)} %get-tuple-element.48), kind=kOutput, calls=%fused_computation.71 | convolution fusion | flops 169869312 | bytes 2482176 | tf_op jit(solution)/shard_map/dot_general | solution.py:412
  (71 shorter events, 11.5 us)
Async XLA Ops:
  0.6 115.0 %copy-start = (bf16[1536,768]{1,0:T(8,128)(2,1)S(1)}, bf16[1536,768]{1,0:T(8,128)(2,1)}, u32[]{:S(2)}) copy-start(bf16[1536,768]{1,0:T(8,128)(2,1)} %param.22) | copy-start | bytes 7077892
  0.6 16.7 %copy-start.2 = (bf16[1,128,768]{2,1,0:T(8,128)(2,1)S(1)}, bf16[1,128,768]{2,1,0:T(8,128)(2,1)}, u32[]{:S(2)}) copy-start(bf16[1,128,768]{2,1,0:T(8,128)(2,1)} %param.14) | copy-start | bytes 589828
  0.7 12.8 %copy-start.16 = (s32[8]{0:T(128)S(1)}, s32[8]{0:T(128)}, u32[]{:S(2)}) copy-start(s32[8]{0:T(128)} %param.18) | copy-start | bytes 100
  0.7 18.3 %collective-permute-start = (bf16[128,768]{1,0:T(8,128)(2,1)}, bf16[128,768]{1,0:T(8,128)(2,1)}, u32[]{:S(2)}, u32[]{:S(2)}) collective-permute-start(bf16[128,768]{1,0:T(8,128)(2,1)} %bitcast.47), channel_id=1, source_target_pairs={{0,32},{32,0},{1,33},{33,1},{2,34},{34,2},{3,35},{35,3},{4,36},{36... | collective-permute-start | bytes 589832 | tf_op jit(solution)/shard_map/ppermute | solution.py:336
  2.1 15.2 %collective-permute-start.1 = (bf16[128,768]{1,0:T(8,128)(2,1)}, bf16[128,768]{1,0:T(8,128)(2,1)}, u32[]{:S(2)}, u32[]{:S(2)}) collective-permute-start(bf16[128,768]{1,0:T(8,128)(2,1)} %bitcast.32), channel_id=1, source_target_pairs={{0,32},{32,0},{1,33},{33,1},{2,34},{34,2},{3,35},{35,3},{4,36},{36... | collective-permute-start | bytes 589832 | tf_op jit(solution)/shard_map/ppermute | solution.py:337
  4.8 24.7 %all-to-all-start = ((bf16[32,120,128]{2,1,0:T(8,128)(2,1)}), bf16[32,120,128]{2,1,0:T(8,128)(2,1)S(1)}, u32[]{:S(2)}, u32[]{:S(2)}) async-start(bf16[32,120,128]{2,1,0:T(8,128)(2,1)} %packed.1), calls=%async_computation | async-start | bytes 1966080 | tf_op jit(solution)/shard_map/all_to_all | solution.py:22
  19.0 3.4 %copy-start.15 = (bf16[1,128,768]{2,1,0:T(8,128)(2,1)S(1)}, bf16[1,128,768]{2,1,0:T(8,128)(2,1)}, u32[]{:S(2)}) copy-start(bf16[1,128,768]{2,1,0:T(8,128)(2,1)} %param.12) | copy-start | bytes 589828
  29.6 0.9 copy-start.6
  52.4 19.3 %all-to-all-start.1 = ((bf16[32,120,128]{2,1,0:T(8,128)(2,1)}), bf16[32,120,128]{2,1,0:T(8,128)(2,1)S(1)}, u32[]{:S(2)}, u32[]{:S(2)}) async-start(bf16[32,120,128]{2,1,0:T(8,128)(2,1)} %attention_grads.1), calls=%async_computation.1 | async-start | bytes 1966080 | tf_op jit(solution)/shard_map/all_to_all | solution.py:22
  56.5 5.1 %copy-start.17 = (s32[1,128,1]{1,2,0:T(1,128)S(1)}, s32[1,128,1]{1,2,0:T(1,128)}, u32[]{:S(2)}) copy-start(s32[1,128,1]{1,2,0:T(1,128)} %param.19) | copy-start | bytes 1540
  56.6 5.3 %copy-start.13 = (bf16[1,256,1536]{2,1,0:T(8,128)(2,1)S(1)}, bf16[1,256,1536]{2,1,0:T(8,128)(2,1)}, u32[]{:S(2)}) copy-start(bf16[1,256,1536]{2,1,0:T(8,128)(2,1)} %param.21) | copy-start | bytes 2359300
  56.6 5.3 %copy-start.14 = (bf16[1,256,1536]{2,1,0:T(8,128)(2,1)S(1)}, bf16[1,256,1536]{2,1,0:T(8,128)(2,1)}, u32[]{:S(2)}) copy-start(bf16[1,256,1536]{2,1,0:T(8,128)(2,1)} %param.20) | copy-start | bytes 2359300
  59.7 4.9 %collective-permute-start.2 = (bf16[1536,256]{1,0:T(8,128)(2,1)S(1)}, bf16[1536,256]{1,0:T(8,128)(2,1)}, u32[]{:S(2)}, u32[]{:S(2)}) collective-permute-start(bf16[1536,256]{1,0:T(8,128)(2,1)S(1)} %fusion.11), channel_id=1, source_target_pairs={{0,32},{32,0},{1,33},{33,1},{2,34},{34,2},{3,35},{35,3},{4,36},{36... | collective-permute-start | bytes 2359304 | tf_op jit(solution)/shard_map/ppermute | solution.py:334
  71.7 1.0 copy-start.1
  77.7 12.7 %copy-start.3 = (bf16[256,768]{1,0:T(8,128)(2,1)S(1)}, bf16[256,768]{1,0:T(8,128)(2,1)}, u32[]{:S(2)}) copy-start(bf16[256,768]{1,0:T(8,128)(2,1)} %pad_maximum_fusion.2) | copy-start | bytes 1179652
  81.6 7.5 %copy-start.8 = (bf16[768,128]{1,0:T(8,128)(2,1)}, bf16[768,128]{1,0:T(8,128)(2,1)S(1)}, u32[]{:S(2)}) copy-start(bf16[768,128]{1,0:T(8,128)(2,1)S(1)} %get-tuple-element.46) | copy-start | bytes 589828
  81.7 6.7 %collective-permute-start.3 = (bf16[768,128]{1,0:T(8,128)(2,1)}, bf16[768,128]{1,0:T(8,128)(2,1)S(1)}, u32[]{:S(2)}, u32[]{:S(2)}) collective-permute-start(bf16[768,128]{1,0:T(8,128)(2,1)} %get-tuple-element.45), channel_id=1, source_target_pairs={{0,32},{32,0},{1,33},{33,1},{2,34},{34,2},{3,35},{35,3},{4,36},{36... | collective-permute-start | bytes 589832 | tf_op jit(solution)/shard_map/ppermute | solution.py:368
  84.4 14.5 %all-to-all-start.2 = ((bf16[32,8,768]{2,1,0:T(8,128)(2,1)}), bf16[32,8,768]{2,1,0:T(8,128)(2,1)S(1)}, u32[]{:S(2)}, u32[]{:S(2)}) async-start(bf16[32,8,768]{2,1,0:T(8,128)(2,1)} %bitcast.41), calls=%async_computation.2 | async-start | bytes 786432 | tf_op jit(solution)/shard_map/all_to_all | solution.py:22
  88.3 0.8 copy-start.11
  90.4 2.4 %copy-start.7 = (bf16[1536,256]{1,0:T(8,128)(2,1)S(1)}, bf16[1536,256]{1,0:T(8,128)(2,1)}, u32[]{:S(2)}) copy-start(bf16[1536,256]{1,0:T(8,128)(2,1)} %fusion.12) | copy-start | bytes 2359300
  90.5 2.4 %copy-start.9 = (bf16[768,128]{1,0:T(8,128)(2,1)S(1)}, bf16[768,128]{1,0:T(8,128)(2,1)}, u32[]{:S(2)}) copy-start(bf16[768,128]{1,0:T(8,128)(2,1)} %copy-done.8) | copy-start | bytes 589828
  90.5 2.4 %copy-start.12 = (bf16[768,128]{1,0:T(8,128)(2,1)S(1)}, bf16[768,128]{1,0:T(8,128)(2,1)}, u32[]{:S(2)}) copy-start(bf16[768,128]{1,0:T(8,128)(2,1)} %copy-done.11) | copy-start | bytes 589828
  92.9 1.3 copy-start.18
  98.9 2.5 %copy-start.4 = (bf16[32,8,768]{2,1,0:T(8,128)(2,1)}, bf16[32,8,768]{2,1,0:T(8,128)(2,1)S(1)}, u32[]{:S(2)}) copy-start(bf16[32,8,768]{2,1,0:T(8,128)(2,1)S(1)} %all-to-all-done.2) | copy-start | bytes 1179652
  98.9 2.5 %collective-permute-start.4 = (bf16[256,768]{1,0:T(8,128)(2,1)S(1)}, bf16[256,768]{1,0:T(8,128)(2,1)S(1)}, u32[]{:S(2)}, u32[]{:S(2)}) collective-permute-start(bf16[256,768]{1,0:T(8,128)(2,1)S(1)} %bitcast.35), channel_id=1, source_target_pairs={{0,32},{32,0},{1,33},{33,1},{2,34},{34,2},{3,35},{35,3},{4,36},{36... | collective-permute-start | bytes 1179656 | tf_op jit(solution)/shard_map/ppermute | solution.py:394
  101.4 0.7 copy-start.10
  107.6 8.0 %copy-start.5 = (bf16[32,8,768]{2,1,0:T(8,128)(2,1)S(1)}, bf16[32,8,768]{2,1,0:T(8,128)(2,1)}, u32[]{:S(2)}) copy-start(bf16[32,8,768]{2,1,0:T(8,128)(2,1)} %copy-done.4) | copy-start | bytes 1179652
  107.6 54.3 %all-to-all-start.3 = ((bf16[64,24,1152]{2,1,0:T(8,128)(2,1)}), bf16[64,24,1152]{2,1,0:T(8,128)(2,1)}, u32[]{:S(2)}, u32[]{:S(2)}) async-start(bf16[64,24,1152]{2,1,0:T(8,128)(2,1)} %bitcast.31), calls=%async_computation.3 | async-start | bytes 7077888 | tf_op jit(solution)/shard_map/all_to_all | solution.py:22
  164.5 2.3 %collective-permute-start.5 = (f32[12,1152]{1,0:T(8,128)S(1)}, f32[12,1152]{1,0:T(8,128)S(1)}, u32[]{:S(2)}, u32[]{:S(2)}) collective-permute-start(f32[12,1152]{1,0:T(8,128)S(1)} %slice_select_fusion.1), channel_id=1, source_target_pairs={{0,32},{32,0},{1,33},{33,1},{2,34},{34,2},{3,35},{35,3},{4,36},{36... | collective-permute-start | bytes 165896 | tf_op jit(solution)/shard_map/ppermute | solution.py:403

commit v3 on v2

v3 whole, which is shorter than its diff:
```python
from functools import partial

import jax
import jax.numpy as jnp
from jax import lax
from jax.experimental import pallas as pl
from jax.experimental.pallas import tpu as pltpu
from jax.sharding import Mesh, PartitionSpec as P

F32 = jnp.float32
BF16 = jnp.bfloat16
DP = ("zh", "co")
SEQ = ("y", "x", "zl")
GRP = ("x", "zl")
ALL = DP + SEQ
KC = 256
LOG2E = 1.4426950408889634


def near(x):
    return pltpu.with_memory_space_constraint(x, pltpu.VMEM)


def exchange(x, axes):
    return lax.all_to_all(x, axes, 0, 0, tiled=True)


def sent_to_all(x, axes):
    n = lax.axis_size(axes)
    return exchange(jnp.broadcast_to(x[None], (n, *x.shape)), axes)


def blocks_turned(srcs, lane, sub, count):
    outs = []
    for a in range(count):
        out = None
        for b in range(count):
            shift = (b - a) % count * sub
            moved = pltpu.roll(srcs[b], shift, 1) if shift else srcs[b]
            out = moved if out is None else jnp.where(lane == b, moved, out)
        outs.append(out)
    return outs


def attention_kernel(
    par, mine, back, kmat, vmat, kt, vt, code, score, prob, dk, dv, *, hd, tok, nkb, ny, scaling
):
    length = nkb * tok
    qb = length // ny
    sub = tok // ny
    part = 2 * hd // ny
    off = par[0]
    inv_len, dil, inv_dil = par[1], par[2], par[3]

    def code_of(pos):
        seg = jnp.floor((pos + 0.5) * inv_len)
        res = pos - dil * jnp.floor((pos + 0.5) * inv_dil)
        return seg * 8.0 + res

    for b in range(nkb):
        kb = mine[b, :hd, :]
        vb = mine[b, hd : 2 * hd, :]
        kt[:, b * tok : (b + 1) * tok] = kb
        vt[:, b * tok : (b + 1) * tok] = vb
        kmat[b * tok : (b + 1) * tok, :] = kb.astype(F32).T.astype(BF16)
        vmat[b * tok : (b + 1) * tok, :] = vb.astype(F32).T.astype(BF16)
        pos = lax.broadcasted_iota(jnp.int32, (tok, 128), 0).astype(F32) + float(b * tok)
        code[b * tok : (b + 1) * tok, :] = code_of(pos)

    nb = qb // sub
    lane = lax.broadcasted_iota(jnp.int32, (part, tok), 1) // sub
    tiles = []
    for first in range(0, nb, ny):
        srcs = [mine[first + y, 2 * hd :, :].astype(F32) for y in range(ny)]
        tiles.append(jnp.concatenate(blocks_turned(srcs, lane, sub, ny), axis=0))
    qd = jnp.concatenate(tiles, axis=1)
    qt = qd[:hd, :].astype(BF16)
    dot_ = qd[hd:, :]
    qidx = lax.broadcasted_iota(jnp.int32, (8, qb), 1).astype(F32)
    qpos = qidx + float(tok - sub) * jnp.floor(qidx * (1.0 / sub)) + off
    qcode = code_of(qpos)[0:1, :]

    mx = jnp.full((8, qb), -3e38, F32)
    for c in range(length // KC):
        rows = slice(c * KC, (c + 1) * KC)
        s = jnp.dot(kmat[rows, :], qt, preferred_element_type=F32)
        ck = code[rows, :]
        s = jnp.where(jnp.concatenate([ck] * (qb // 128), axis=1) == qcode, s, -1e30)
        score[rows, :] = s
        mx = jnp.maximum(mx, jnp.max(s.reshape(KC // 8, 8, qb), axis=0))
    top = jnp.max(mx, axis=0, keepdims=True)

    tot = jnp.zeros((8, qb), F32)
    ot = jnp.zeros((hd, qb), F32)
    for c in range(length // KC):
        rows = slice(c * KC, (c + 1) * KC)
        p = jnp.exp2((score[rows, :] - top) * (scaling * LOG2E))
        tot = tot + jnp.sum(p.reshape(KC // 8, 8, qb), axis=0)
        ph = p.astype(BF16)
        prob[rows, :] = ph
        ot = ot + jnp.dot(vt[:, rows], ph, preferred_element_type=F32)
    inv = 1.0 / jnp.sum(tot, axis=0, keepdims=True)
    ot = ot * inv
    dn = dot_ * inv
    dnh = dn.astype(BF16)
    delta = jnp.sum(dnh.astype(F32) * ot, axis=0, keepdims=True)
    dmat = dn.T.astype(BF16)
    qmat = qt.astype(F32).T.astype(BF16)

    dqt = jnp.zeros((hd, qb), F32)
    for c in range(length // KC):
        rows = slice(c * KC, (c + 1) * KC)
        ph = prob[rows, :]
        dp = jnp.dot(vmat[rows, :], dnh, preferred_element_type=F32)
        ds = (ph.astype(F32) * (dp - delta)).astype(BF16)
        dv[rows, :] = jnp.dot(ph, dmat, preferred_element_type=F32)
        dk[rows, :] = jnp.dot(ds, qmat, preferred_element_type=F32)
        dqt = dqt + jnp.dot(kt[:, rows], ds, preferred_element_type=F32)

    both = jnp.concatenate([dqt * scaling, ot], axis=0)
    for first in range(0, nb, ny):
        cols = slice(first * sub, (first + ny) * sub)
        srcs = [both[g * part : (g + 1) * part, cols] for g in range(ny)]
        for y, block in enumerate(blocks_turned(srcs, lane, sub, ny)):
            back[first + y, 2 * hd :, :] = block.astype(BF16)

    for b in range(nkb):
        rows = slice(b * tok, (b + 1) * tok)
        back[b, :hd, :] = (dk[rows, :].T * scaling).astype(BF16)
        back[b, hd : 2 * hd, :] = dv[rows, :].T.astype(BF16)


def attention_grads(par, mine, hd, ny, scaling):
    nkb, rows, tok = mine.shape
    length = nkb * tok
    qb = length // ny
    whole = pl.BlockSpec(memory_space=pltpu.VMEM)
    return pl.pallas_call(
        partial(attention_kernel, hd=hd, tok=tok, nkb=nkb, ny=ny, scaling=scaling),
        out_shape=pltpu.VMEM((nkb, rows, tok), BF16),
        in_specs=[pl.BlockSpec(memory_space=pltpu.SMEM), whole],
        out_specs=whole,
        scratch_shapes=[
            pltpu.VMEM((length, hd), BF16),
            pltpu.VMEM((length, hd), BF16),
            pltpu.VMEM((hd, length), BF16),
            pltpu.VMEM((hd, length), BF16),
            pltpu.VMEM((length, 128), F32),
            pltpu.VMEM((length, qb), F32),
            pltpu.VMEM((length, qb), BF16),
            pltpu.VMEM((length, hd), F32),
            pltpu.VMEM((length, hd), F32),
        ],
        cost_estimate=pl.CostEstimate(
            flops=30_000_000_000, bytes_accessed=4_000_000, transcendentals=length * length // ny
        ),
        name="attention_grads",
    )(par, near(mine))


def pack_kernel(saved, cot, weight, out, *, heads, hd, tok, ny):
    sub = tok // ny
    part = 2 * hd // ny
    width = heads * hd
    grads = lax.dot_general(
        weight[...], cot[...], (((1,), (1,)), ((), ())), preferred_element_type=F32
    )
    grads = grads.astype(BF16).astype(F32)
    saved_t = saved[...].astype(F32).T
    lane = lax.broadcasted_iota(jnp.int32, (part, tok), 1) // sub
    for h in range(heads):
        rows = slice(h * hd, (h + 1) * hd)
        keys = saved_t[width + h * hd : width + (h + 1) * hd, :].astype(BF16)
        values = saved_t[2 * width + h * hd : 2 * width + (h + 1) * hd, :].astype(BF16)
        both = jnp.concatenate([saved_t[rows, :], grads[rows, :]], axis=0)
        srcs = [both[g * part : (g + 1) * part, :] for g in range(ny)]
        for y, block in enumerate(blocks_turned(srcs, lane, sub, ny)):
            out[y * heads + h, :hd, :] = keys
            out[y * heads + h, hd : 2 * hd, :] = values
            out[y * heads + h, 2 * hd :, :] = block.astype(BF16)


def packed(saved, cot, weight, heads, ny):
    tok = saved.shape[0]
    hd = weight.shape[0] // heads
    rows = 2 * hd + 2 * hd // ny
    return pl.pallas_call(
        partial(pack_kernel, heads=heads, hd=hd, tok=tok, ny=ny),
        out_shape=jax.ShapeDtypeStruct((ny * heads, rows, tok), BF16),
        cost_estimate=pl.CostEstimate(
            flops=2 * weight.size * tok, bytes_accessed=2_000_000, transcendentals=0
        ),
        in_specs=[pl.BlockSpec(memory_space=pltpu.VMEM)] * 3,
        out_specs=pl.BlockSpec(memory_space=pltpu.VMEM),
        name="packed",
    )(saved, cot, weight)


def token_kernel(core, got, cot_t, weight, selector, routed, own, send, grads, *, heads, hd, ny):
    tok = got.shape[2]
    sub = tok // ny
    part = 2 * hd // ny
    width = heads * hd
    lane = lax.broadcasted_iota(jnp.int32, (part, tok), 1) // sub
    for h in range(heads):
        total = got[h, : 2 * hd, :].astype(F32)
        for y in range(1, ny):
            total = total + got[y * heads + h, : 2 * hd, :].astype(F32)
        total = total.astype(BF16)
        srcs = [got[y * heads + h, 2 * hd :, :].astype(F32) for y in range(ny)]
        both = jnp.concatenate(blocks_turned(srcs, lane, sub, ny), axis=0).astype(BF16)
        rows = [slice(i * width + h * hd, i * width + (h + 1) * hd) for i in range(4)]
        grads[rows[0], :] = both[:hd, :]
        grads[rows[1], :] = total[:hd, :]
        grads[rows[2], :] = total[hd:, :]
        grads[rows[3], :] = both[hd:, :]
    embed_t = jnp.dot(weight[...], grads[: 3 * width, :], preferred_element_type=F32)
    embed_t = (cot_t[...].astype(F32) + embed_t).astype(BF16)
    routed[...] = lax.dot_general(
        selector[...], embed_t, (((1,), (1,)), ((), ())), preferred_element_type=F32
    ).astype(BF16)

    @pl.when(core[0] == 0)
    def _():
        own[...] = grads[: 2 * width, :]
        send[...] = grads[2 * width :, :]

    @pl.when(core[0] != 0)
    def _():
        own[...] = grads[2 * width :, :]
        send[...] = grads[: 2 * width, :]


def token_grads(core, got, cot_t, weight, selector, heads, hd, ny):
    d_slide, tok = cot_t.shape
    vmem = pl.BlockSpec(memory_space=pltpu.VMEM)
    return pl.pallas_call(
        partial(token_kernel, heads=heads, hd=hd, ny=ny),
        out_shape=(
            jax.ShapeDtypeStruct((selector.shape[0], d_slide), BF16),
            jax.ShapeDtypeStruct((2 * heads * hd, tok), BF16),
            jax.ShapeDtypeStruct((2 * heads * hd, tok), BF16),
        ),
        in_specs=[pl.BlockSpec(memory_space=pltpu.SMEM)] + [vmem] * 4,
        out_specs=(vmem, vmem, vmem),
        scratch_shapes=[pltpu.VMEM((4 * heads * hd, tok), BF16)],
        cost_estimate=pl.CostEstimate(
            flops=2 * weight.size * tok, bytes_accessed=4_000_000, transcendentals=0
        ),
        name="token_grads",
    )(core, near(got), near(cot_t), near(weight), near(selector))


def final_kernel(core, mine, pair, weight_t, proj, embed, qkv, out, *, half):
    d_slide = weight_t.shape[0]
    o_half = half // 2
    low = core[0] == 0
    a, b = mine[...], pair[...]
    from_low = jnp.where(low, a, b)
    from_high = jnp.where(low, b, a)
    embed[...] = from_low[:, :d_slide]
    wide = (from_low.shape[1] - d_slide)
    qkv[:, :wide] = from_low[:half, d_slide:]
    qkv[:, wide : 2 * wide] = from_low[half:, d_slide:]
    qkv[:, 2 * wide :] = from_high[:half, d_slide:]
    out[:, :wide] = from_high[half : half + o_half, d_slide:]
    out[:, wide:] = from_high[half + o_half :, d_slide:]
    factor = from_high[:, :d_slide]
    first = factor.astype(BF16)
    rest = factor - first.astype(F32)
    second = rest.astype(BF16)
    third = (rest - second.astype(F32)).astype(BF16)
    total = jnp.dot(first, weight_t[...], preferred_element_type=F32)
    total = total + jnp.dot(second, weight_t[...], preferred_element_type=F32)
    proj[...] = total + jnp.dot(third, weight_t[...], preferred_element_type=F32)


def final_outputs(core, mine, pair, weight_t):
    per, wide = mine.shape
    d_slide, d_tile = weight_t.shape
    half = per // 2
    vmem = pl.BlockSpec(memory_space=pltpu.VMEM)
    return pl.pallas_call(
        partial(final_kernel, half=half),
        out_shape=(
            jax.ShapeDtypeStruct((per, d_tile), F32),
            jax.ShapeDtypeStruct((per, d_slide), F32),
            jax.ShapeDtypeStruct((half, 3 * (wide - d_slide)), F32),
            jax.ShapeDtypeStruct((half // 2, 2 * (wide - d_slide)), F32),
        ),
        in_specs=[pl.BlockSpec(memory_space=pltpu.SMEM)] + [vmem] * 3,
        out_specs=(vmem, vmem, vmem, vmem),
        cost_estimate=pl.CostEstimate(
            flops=6 * per * weight_t.size, bytes_accessed=3_000_000, transcendentals=0
        ),
        name="final_outputs",
    )(core, near(mine), near(pair), near(weight_t))


def summed_kernel(rows, incoming, swapped, small, out, both):
    slots, d_slide = incoming.shape

    @pl.when(pl.program_id(0) == 0)
    def _():
        both[:slots, :] = incoming[...]
        both[slots:, :] = swapped[...]

    out[:, :d_slide] = jnp.dot(rows[...], both[...], preferred_element_type=F32).astype(BF16)
    out[:, d_slide:] = small[...]


def summed_terms(rows, incoming, swapped, small):
    count, depth = rows.shape
    slots, d_slide = incoming.shape
    block = 512
    wide = d_slide + small.shape[1]
    vmem = pl.BlockSpec(memory_space=pltpu.VMEM)
    return pl.pallas_call(
        summed_kernel,
        grid=(count // block,),
        out_shape=jax.ShapeDtypeStruct((count, wide), BF16),
        in_specs=[
            pl.BlockSpec((block, depth), lambda i: (i, 0)),
            vmem,
            vmem,
            pl.BlockSpec((block, small.shape[1]), lambda i: (i, 0)),
        ],
        out_specs=pl.BlockSpec((block, wide), lambda i: (i, 0)),
        scratch_shapes=[pltpu.VMEM((depth, d_slide), BF16)],
        compiler_params=pltpu.CompilerParams(dimension_semantics=("arbitrary",)),
        cost_estimate=pl.CostEstimate(
            flops=2 * count * depth * d_slide, bytes_accessed=8_000_000, transcendentals=0
        ),
        name="summed_terms",
    )(rows, near(incoming), near(swapped), small)


def one_hot_rows(source, width, keep=None):
    hit = source[:, None] == jnp.arange(width, dtype=jnp.int32)[None, :]
    if keep is not None:
        hit = hit & keep[:, None]
    return hit.astype(BF16)


def picked_rows(onehot, x):
    return jnp.einsum("rx,tx->rt", onehot, x, preferred_element_type=F32).astype(BF16)


def local(
    tile_embed,
    qkv_saved,
    out_cotangent,
    qkv_weight,
    out_weight,
    seg_length,
    dilation,
    owner_map,
    tile_hidden,
    tile_output,
    embed_weight,
    proj_weight,
):
    heads = seg_length.shape[0]
    width = out_weight.shape[0]
    hd = width // heads
    tok = qkv_saved.shape[1]
    d_slide = tile_embed.shape[2]
    n_seq = lax.axis_size(SEQ)
    n_y = lax.axis_size("y")
    n_dp = lax.axis_size(DP)
    n_dev = n_dp * n_seq
    scaling = hd ** (-0.5)
    cot = out_cotangent[0]
    head = lax.axis_index(GRP)
    core = lax.axis_index("co")

    destination = owner_map[0, :, 0]
    capacity = tile_hidden.shape[1] // n_seq
    onehot = (destination[:, None] == jnp.arange(n_seq, dtype=jnp.int32)[None, :]).astype(F32)
    lower = (
        jnp.arange(tok, dtype=jnp.int32)[:, None] > jnp.arange(tok, dtype=jnp.int32)[None, :]
    ).astype(BF16)
    before = jnp.dot(lower, onehot.astype(BF16), preferred_element_type=F32)
    rank = jnp.sum(before * onehot, axis=1).astype(jnp.int32)
    slot_index = destination * capacity + rank
    selector = (
        jnp.arange(n_seq * capacity, dtype=jnp.int32)[:, None] == slot_index[None, :]
    ).astype(BF16)
    core_of = core.astype(jnp.int32).reshape(1)
    outgoing = packed(qkv_saved[0], cot, out_weight, heads, n_y)
    outgoing, hidden_rows, output_rows, cot_later = lax.optimization_barrier(
        (outgoing, tile_hidden[0], tile_output[0], cot)
    )
    cot_t = cot_later.T
    mine = exchange(outgoing, SEQ)

    seg = seg_length[head].astype(F32)
    dil = dilation[head].astype(F32)
    off = (lax.axis_index("y") * (tok // n_y)).astype(F32)
    par = jnp.stack([off, 1.0 / seg, dil, 1.0 / dil])
    back = attention_grads(par, mine, hd, n_y, scaling)

    swap = partial(lax.ppermute, axis_name="co", perm=[(0, 1), (1, 0)])
    low = core == 0
    d_tile = embed_weight.shape[0]
    holders = n_dev // 2
    per = d_tile // n_dev
    half = per // 2
    row = jnp.arange(d_tile, dtype=jnp.int32)
    holder = row // (2 * per)
    to_core = row // per % 2
    owner = (holder // n_seq * 2 + to_core) * n_seq + holder % n_seq
    second = row // half % 2 == 1
    spot = row % half
    tile_spots = one_hot_rows(owner * per + row % per, d_tile)
    keep = picked_rows(tile_spots, jnp.where(low, output_rows, hidden_rows))
    other = swap(picked_rows(tile_spots, jnp.where(low, hidden_rows, output_rows)))
    embed_rows = tile_embed[0]
    embed_pair = jnp.concatenate([embed_rows, swap(embed_rows)], axis=0)
    cot_pair = jnp.concatenate([cot, swap(cot)], axis=0)
    first_rows = picked_rows(one_hot_rows(owner * half + spot, d_slide, ~second), embed_pair)
    second_rows = picked_rows(one_hot_rows(owner * half + spot, d_slide, second), embed_pair)
    back, first_rows, second_rows, cot_pair, cot_t, selector = lax.optimization_barrier(
        (back, first_rows, second_rows, cot_pair, cot_t, selector)
    )
    tile_rows = jnp.concatenate([keep, other], axis=1)
    got, tile_rows = lax.optimization_barrier((exchange(back, SEQ), tile_rows))
    routed, own, send = token_grads(core_of, got, cot_t, qkv_weight, selector, heads, hd, n_y)
    incoming = exchange(routed.reshape(n_seq, capacity, d_slide), SEQ).reshape(-1, d_slide)
    grads = jnp.concatenate([own, swap(send)], axis=1)
    grads = grads.reshape(2, width, 2 * tok)
    o_half = half // 2
    att_row = owner * o_half + spot % o_half
    att_low = jnp.einsum(
        "ra,at->rt",
        one_hot_rows(att_row, width, second & (spot < o_half)),
        grads[1],
        preferred_element_type=F32,
    ).astype(BF16)
    att_high = jnp.einsum(
        "ra,at->rt",
        one_hot_rows(att_row, width, second & (spot >= o_half)),
        grads[1],
        preferred_element_type=F32,
    ).astype(BF16)
    left_side = jnp.concatenate(
        [first_rows, jnp.where(low, second_rows, att_low), jnp.where(low, 0, att_high)], axis=1
    )
    flat = grads.transpose(0, 2, 1)
    right_side = jnp.concatenate(
        [flat[0], jnp.where(low, flat[1], cot_pair[:, :width]), cot_pair[:, width:]], axis=0
    )
    small = jnp.dot(left_side, right_side, preferred_element_type=F32).astype(BF16)
    incoming, small = lax.optimization_barrier((incoming, small))

    term = summed_terms(tile_rows, incoming, swap(incoming), small)
    term = term.reshape(holders, -1, term.shape[1])
    held = jnp.sum(exchange(term, ("zh",) + SEQ).astype(F32), axis=0)
    tile_grad = jnp.einsum("sd,ed->se", incoming, embed_weight, preferred_element_type=F32)
    hidden_grad = jnp.einsum(
        "se,fe->sf", tile_grad.astype(BF16), proj_weight, preferred_element_type=F32
    ).astype(BF16)[None]
    held, hidden_grad, weight_t = lax.optimization_barrier((held, hidden_grad, embed_weight.T))
    mine_held = jnp.where(low, held[:per], held[per:])
    pair_held = swap(jnp.where(low, held[per:], held[:per]))
    proj_sum, embed_sum, qkv_sum, out_sum = final_outputs(core_of, mine_held, pair_held, weight_t)
    return (hidden_grad, proj_sum, embed_sum, qkv_sum, out_sum)


def solution(mesh):
    fine = Mesh(mesh.devices.reshape(2, 2, 4, 4, 2), ALL)
    part = P(DP, SEQ, None)
    rows = P(ALL, None)
    return jax.shard_map(
        local,
        mesh=fine,
        in_specs=(part, part, part, P(), P(), P(), P(), part, part, part, P(), P()),
        out_specs=(part, rows, rows, rows, rows),
        check_vma=False,
    )
```

time: 172 us -> 158 us (0.919)
  matrix products: 29.7 us -> 23.5 us
  Pallas kernels: 32.2 us -> 29.1 us
  other arithmetic: 8.78 us -> 6.01 us
    dot_general x2 -> x0, matrix products: 5.86 us -> none  [the longest x1 3.28 us: local(): jnp.dot(selector, embed_grad, preferred_element_type=F32).astype(BF16)]
    pallas_call x1, Pallas kernels: 21.9 us -> 17.6 us  [attention_grads(): pl.pallas_call(partial(attention_kernel, hd=hd, tok=tok, nkb=nkb, ny=ny,...]
    unnamed x38 -> x21, local copies, waits for them, and re-layouts: 2.7 us -> 6.01 us
    ppermute x3, starting transfers between devices: 5.82 us -> 3.28 us  [the longest x1 1.43 us: local(): grads = jnp.concatenate([own, swap(send)], axis=1)]
    slice x6 -> x0, local copies, waits for them, and re-layouts: 2.48 us -> none  [the longest x2 1.84 us: local(): query_key, value_t = (qkv_grad_t[:2 * width], qkv_grad_t[2 * width:])]
    pallas_call x2 -> x3, Pallas kernels: 7.67 us -> 8.85 us  [the longest x1 5.24 us: summed_terms(): pl.pallas_call(summed_kernel, grid=(count // block,), out_shape=jax.Shape...]
  transfers between devices with their start and end apart: 10 -> 10, of which waited for: 6 -> 6; matrix products, arithmetic and copies ran while one was open for 18% -> 20% of each run, Pallas kernels for 2% -> 13%
where the time goes in v3:
time: 158 us; the launch traced here: 156 us
  waiting for transfers between devices  56.7 us (36%)
  starting transfers between devices  31.6 us (20%)
  Pallas kernels  29.1 us (18%)
  matrix products  23.5 us (15%)
  local copies, waits for them, and re-layouts  7.25 us (5%)
  other arithmetic  6.01 us (4%)
  between operations  2.34 us (1%)
    all_to_all x4, waiting for transfers between devices, exchange(): return lax.all_to_all(x, axes, 0, 0, tiled=True)  54.4 us
    all_to_all x4, starting transfers between devices, exchange(): return lax.all_to_all(x, axes, 0, 0, tiled=True)  25.3 us
    pallas_call x1, Pallas kernels, attention_grads(): pl.pallas_call(partial(attention_kernel, hd=hd, tok=tok, nkb=nkb, ny=ny,...  17.6 us
    dot_general x4, matrix products, picked_rows(): jnp.einsum('rx,tx->rt', onehot, x, preferred_element_type=F32).astype(BF16)  12.3 us
    unnamed x21, local copies, waits for them, and re-layouts  6.01 us
    dot_general x1, matrix products, local(): jnp.einsum('se,fe->sf', tile_grad.astype(BF16), proj_weight, preferred_el...  5.97 us
    pallas_call x1, Pallas kernels, summed_terms(): pl.pallas_call(summed_kernel, grid=(count // block,), out_shape=jax.Shape...  5.24 us
  transfers between devices with their start and end apart: 10, of which 6 were waited for; matrix products, arithmetic and copies ran while one was open for 20% of the time, Pallas kernels for 13%

profile of v3, /device:TPU:1, one launch (start us, length us, event | category | flops | bytes accessed | tf_op | source)
XLA Modules:
  0.0 156.4 jit_solution(8157926637332185291)
XLA Ops:
  0.7 1.2 copy.17
  1.9 1.5 collective-permute-start.1
  3.4 2.6 %packed.1 = bf16[32,120,128]{2,1,0:T(8,128)(2,1)} custom-call(bf16[128,1152]{1,0:T(8,128)(2,1)} %bitcast.41, bf16[128,768]{1,0:T(8,128)(2,1)} %bitcast.39, bf16[384,768]{1,0:T(8,128)(2,1)} %weight.2), custom_call_target="tpu_custom_call" | custom-call | flops 75497472 | bytes 2000000 | tf_op jit(solution)/shard_map/packed/pallas_call | solution.py:187
  6.0 8.5 %all-to-all-start = ((bf16[32,120,128]{2,1,0:T(8,128)(2,1)}), bf16[32,120,128]{2,1,0:T(8,128)(2,1)S(1)}, u32[]{:S(2)}, u32[]{:S(2)}) async-start(bf16[32,120,128]{2,1,0:T(8,128)(2,1)} %packed.1), calls=%async_computation | async-start | bytes 1966080 | tf_op jit(solution)/shard_map/all_to_all | solution.py:25
  14.7 2.7 %fusion.11 = bf16[1536,256]{1,0:T(8,128)(2,1)} fusion(s32[1536]{0:T(1024)S(1)} %fusion.77, bf16[256,1536]{1,0:T(8,128)(2,1)S(1)} %bitcast.43, bf16[256,1536]{1,0:T(8,128)(2,1)S(1)} %bitcast.45, pred[]{:T(512)S(6)} %eq.143), kind=kOutput, calls=%fused_computation.14 | convolution fusion | flops 1211105280 | bytes 2365441 | tf_op jit(solution)/shard_map/rx,tx->rt/dot_general | solution.py:346
  21.7 3.4 %fusion.12 = bf16[1536,256]{1,0:T(8,128)(2,1)} fusion(s32[1536]{0:T(1024)S(1)} %fusion.74, pred[1536]{0:T(1024)(128)(4,1)S(1)} %fusion.69, bf16[128,768]{1,0:T(8,128)(2,1)} %collective-permute-done, bf16[128,768]{1,0:T(8,128)(2,1)} %bitcast.47), kind=kOutput, calls=%fused_computation.15 | convolution fusion | flops 607518720 | bytes 1187328 | tf_op jit(solution)/shard_map/rx,tx->rt/dot_general | solution.py:346
  25.0 3.2 %fusion.15 = bf16[1536,256]{1,0:T(8,128)(2,1)} fusion(s32[1536]{0:T(1024)S(1)} %fusion.74, pred[1536]{0:T(1024)(128)(4,1)S(1)} %fusion.89, bf16[128,768]{1,0:T(8,128)(2,1)} %collective-permute-done, bf16[128,768]{1,0:T(8,128)(2,1)S(1)} %bitcast.48), kind=kOutput, calls=%fused_computation.16 | convolution fusion | flops 607518720 | bytes 1187328 | tf_op jit(solution)/shard_map/rx,tx->rt/dot_general | solution.py:346
  28.3 2.5 %all-to-all-done.mine = bf16[32,120,128]{2,1,0:T(8,128)(2,1)S(1)} async-done(((bf16[32,120,128]{2,1,0:T(8,128)(2,1)}), bf16[32,120,128]{2,1,0:T(8,128)(2,1)S(1)}, u32[]{:S(2)}, u32[]{:S(2)}) %all-to-all-start) | async-done | bytes 983072 | tf_op jit(solution)/shard_map/all_to_all | solution.py:25
  30.8 17.6 %attention_grads.1 = bf16[32,120,128]{2,1,0:T(8,128)(2,1)} custom-call(f32[4]{0:T(128)} %pad_maximum_fusion.5.par, bf16[32,120,128]{2,1,0:T(8,128)(2,1)S(1)} %all-to-all-done.mine), custom_call_target="tpu_custom_call" | custom-call | flops 30000001024 | bytes 4000000 | tf_op jit(solution)/shard_map/attention_grads/pallas_call | solution.py:138
  48.4 5.5 %all-to-all-start.1 = ((bf16[32,120,128]{2,1,0:T(8,128)(2,1)}), bf16[32,120,128]{2,1,0:T(8,128)(2,1)S(1)}, u32[]{:S(2)}, u32[]{:S(2)}) async-start(bf16[32,120,128]{2,1,0:T(8,128)(2,1)} %attention_grads.1), calls=%async_computation.1 | async-start | bytes 1966080 | tf_op jit(solution)/shard_map/all_to_all | solution.py:25
  53.9 3.0 %fusion.10 = bf16[1536,256]{1,0:T(8,128)(2,1)S(1)} fusion(s32[1536]{0:T(1024)S(1)} %fusion.77, bf16[256,1536]{1,0:T(8,128)(2,1)} %bitcast.44, bf16[256,1536]{1,0:T(8,128)(2,1)} %bitcast.42, pred[]{:T(512)S(6)} %eq.143), kind=kOutput, calls=%fused_computation.13 | convolution fusion | flops 1211105280 | bytes 2365441 | tf_op jit(solution)/shard_map/rx,tx->rt/dot_general | solution.py:346
  57.0 2.5 %pad_maximum_fusion.rows = bf16[1536,512]{1,0:T(8,128)(2,1)} fusion(bf16[1536,256]{1,0:T(8,128)(2,1)} %collective-permute-done.2, bf16[1536,256]{1,0:T(8,128)(2,1)S(1)} %fusion.10), kind=kLoop, calls=%fused_computation.34 | loop fusion | flops 3145728 | bytes 3145728 | tf_op jit(solution)/shard_map/concatenate | solution.py:426
  59.5 11.0 %all-to-all-done.1.got = bf16[32,120,128]{2,1,0:T(8,128)(2,1)S(1)} async-done(((bf16[32,120,128]{2,1,0:T(8,128)(2,1)}), bf16[32,120,128]{2,1,0:T(8,128)(2,1)S(1)}, u32[]{:S(2)}, u32[]{:S(2)}) %all-to-all-start.1) | async-done | bytes 983072 | tf_op jit(solution)/shard_map/all_to_all | solution.py:25
  70.5 1.9 %token_grads.1 = (bf16[256,768]{1,0:T(8,128)(2,1)}, bf16[768,128]{1,0:T(8,128)(2,1)}, bf16[768,128]{1,0:T(8,128)(2,1)}) custom-call(s32[1]{0:T(128)} %bitcast.9.core, bf16[32,120,128]{2,1,0:T(8,128)(2,1)S(1)} %all-to-all-done.1.got, bf16[768,128]{1,0:T(8,128)(2,1)S(1)} %bitcast.32, bf16[768,1152]{1,0:T(8,128)(2,1)S(1)} %copy-done, ...), custom_call_target="tpu_custom_call" | custom-call | flops 226492416 | bytes 4000000 | tf_op jit(solution)/shard_map/token_grads/pallas_call | solution.py:237
  72.5 1.4 collective-permute-start.3
  73.9 3.9 %all-to-all-start.2 = ((bf16[32,8,768]{2,1,0:T(8,128)(2,1)}), bf16[32,8,768]{2,1,0:T(8,128)(2,1)S(1)}, u32[]{:S(2)}, u32[]{:S(2)}) async-start(bf16[32,8,768]{2,1,0:T(8,128)(2,1)} %bitcast.40), calls=%async_computation.2 | async-start | bytes 786432 | tf_op jit(solution)/shard_map/all_to_all | solution.py:25
  77.8 1.0 constant_dynamic-update-slice_fusion.1
  78.9 1.3 fusion.18
  80.2 1.3 convolution_convert_fusion.4
  81.6 1.0 copy-done.8
  82.6 2.5 %convolution_convert_fusion.small = bf16[1536,384]{1,0:T(8,128)(2,1)} fusion(bf16[1536,256]{1,0:T(8,128)(2,1)S(1)} %fusion.18, bf16[1536,256]{1,0:T(8,128)(2,1)S(1)} %broadcast_select_fusion, bf16[1536,256]{1,0:T(8,128)(2,1)S(1)} %copy-done.8, bf16[256,384]{0,1:T(8,128)(2,1)S(1)} %get-tuple-element.54, bf16[256,384]{0,1:T(8,128)(2,1)S(1)} %get-tuple-element.53, ...), kind=kOutput, calls=%fused_computation.11 | convolution fusion | flops 915406848 | bytes 4128768 | tf_op jit(solution)/shard_map/dot_general | solution.py:453
  85.1 3.4 %all-to-all-done.2 = bf16[32,8,768]{2,1,0:T(8,128)(2,1)S(1)} async-done(((bf16[32,8,768]{2,1,0:T(8,128)(2,1)}), bf16[32,8,768]{2,1,0:T(8,128)(2,1)S(1)}, u32[]{:S(2)}, u32[]{:S(2)}) %all-to-all-start.2) | async-done | bytes 393248 | tf_op jit(solution)/shard_map/all_to_all | solution.py:25
  88.4 1.2 collective-permute-start.4
  89.6 1.3 collective-permute-done.4.swapped
  90.9 5.2 %summed_terms.1 = bf16[1536,1152]{1,0:T(8,128)(2,1)} custom-call(bf16[1536,512]{1,0:T(8,128)(2,1)} %pad_maximum_fusion.rows, bf16[256,768]{1,0:T(8,128)(2,1)S(1)} %bitcast.34, bf16[256,768]{1,0:T(8,128)(2,1)S(1)} %collective-permute-done.4.swapped, bf16[1536,384]{1,0:T(8,128)(2,1)} %convolution_convert_fusion.small), custom_call_target="tpu_custom_call" | custom-call | flops 1207959552 | bytes 8000000 | tf_op jit(solution)/shard_map/summed_terms/pallas_call | solution.py:318
  96.2 7.5 %all-to-all-start.3 = ((bf16[64,24,1152]{2,1,0:T(8,128)(2,1)}), bf16[64,24,1152]{2,1,0:T(8,128)(2,1)}, u32[]{:S(2)}, u32[]{:S(2)}) async-start(bf16[64,24,1152]{2,1,0:T(8,128)(2,1)} %bitcast.36), calls=%async_computation.3 | async-start | bytes 7077888 | tf_op jit(solution)/shard_map/all_to_all | solution.py:25
  103.7 2.8 %copy.20 = bf16[1536,768]{0,1:T(8,128)(2,1)S(1)} copy(bf16[1536,768]{1,0:T(8,128)(2,1)} %param.22) | data formatting | bytes 4718592 | tf_op args[10]
  106.5 6.0 %fusion.19 = bf16[1,256,1536]{2,1,0:T(8,128)(2,1)} fusion(bf16[1536,1536]{1,0:T(8,128)(2,1)} %param.23, bf16[256,768]{1,0:T(8,128)(2,1)S(1)} %bitcast.35, bf16[1536,768]{1,0:T(8,128)(2,1)} %param.22), kind=kOutput, calls=%fused_computation.21 | convolution fusion | flops 1812725760 | bytes 8257536 | tf_op jit(solution)/shard_map/se,fe->sf/dot_general | solution.py:460
  112.5 37.4 %all-to-all-done.3 = bf16[64,24,1152]{2,1,0:T(8,128)(2,1)} async-done(((bf16[64,24,1152]{2,1,0:T(8,128)(2,1)}), bf16[64,24,1152]{2,1,0:T(8,128)(2,1)}, u32[]{:S(2)}, u32[]{:S(2)}) %all-to-all-start.3) | async-done | bytes 3538976 | tf_op jit(solution)/shard_map/all_to_all | solution.py:25
  149.9 2.5 %convert_reduce_fusion = f32[24,1152]{1,0:T(8,128)S(1)} fusion(bf16[64,24,1152]{2,1,0:T(8,128)(2,1)} %all-to-all-done.3), kind=kLoop, calls=%fused_computation.3 | loop fusion | flops 3511296 | bytes 3649536 | tf_op jit(solution)/shard_map/reduce_sum | solution.py:458
  152.5 1.4 collective-permute-start.5
  154.8 1.7 %final_outputs.1 = (f32[12,1536]{1,0:T(8,128)}, f32[12,768]{1,0:T(8,128)}, f32[6,1152]{1,0:T(8,128)}, f32[3,768]{1,0:T(4,128)}) custom-call(s32[1]{0:T(128)} %bitcast.9.core, f32[12,1152]{1,0:T(8,128)S(1)} %get-tuple-element.56.mine, f32[12,1152]{1,0:T(8,128)S(1)} %collective-permute-done.5.pair, bf16[768,1536]{1,0:T(8,128)(2,1)S(1)} %bitcast.29), custom_call_target="tpu_custom_call" | custom-call | flops 84934656 | bytes 3000000 | tf_op jit(solution)/shard_map/final_outputs/pallas_call | solution.py:283
  (43 shorter events, 4.1 us)
Async XLA Ops:
  0.6 14.0 %copy-start.3 = (bf16[1,256,1536]{2,1,0:T(8,128)(2,1)S(1)}, bf16[1,256,1536]{2,1,0:T(8,128)(2,1)}, u32[]{:S(2)}) copy-start(bf16[1,256,1536]{2,1,0:T(8,128)(2,1)} %param.21) | copy-start | bytes 2359300
  0.6 14.0 %copy-start.2 = (bf16[1,256,1536]{2,1,0:T(8,128)(2,1)S(1)}, bf16[1,256,1536]{2,1,0:T(8,128)(2,1)}, u32[]{:S(2)}) copy-start(bf16[1,256,1536]{2,1,0:T(8,128)(2,1)} %param.20) | copy-start | bytes 2359300
  1.9 19.7 %collective-permute-start.1 = (bf16[128,768]{0,1:T(8,128)(2,1)S(1)}, bf16[128,768]{0,1:T(8,128)(2,1)S(1)}, u32[]{:S(2)}, u32[]{:S(2)}) collective-permute-start(bf16[128,768]{0,1:T(8,128)(2,1)S(1)} %bitcast.30), channel_id=1, source_target_pairs={{0,32},{32,0},{1,33},{33,1},{2,34},{34,2},{3,35},{35,3},{4,36},{36... | collective-permute-start | bytes 589832 | tf_op jit(solution)/shard_map/ppermute | solution.py:420
  3.3 18.3 %collective-permute-start = (bf16[128,768]{1,0:T(8,128)(2,1)}, bf16[128,768]{1,0:T(8,128)(2,1)}, u32[]{:S(2)}, u32[]{:S(2)}) collective-permute-start(bf16[128,768]{1,0:T(8,128)(2,1)} %bitcast.46), channel_id=1, source_target_pairs={{0,32},{32,0},{1,33},{33,1},{2,34},{34,2},{3,35},{35,3},{4,36},{36... | collective-permute-start | bytes 589832 | tf_op jit(solution)/shard_map/ppermute | solution.py:419
  6.0 24.8 %all-to-all-start = ((bf16[32,120,128]{2,1,0:T(8,128)(2,1)}), bf16[32,120,128]{2,1,0:T(8,128)(2,1)S(1)}, u32[]{:S(2)}, u32[]{:S(2)}) async-start(bf16[32,120,128]{2,1,0:T(8,128)(2,1)} %packed.1), calls=%async_computation | async-start | bytes 1966080 | tf_op jit(solution)/shard_map/all_to_all | solution.py:25
  14.6 3.5 %copy-start.5 = (s32[1,128,1]{1,2,0:T(1,128)S(1)}, s32[1,128,1]{1,2,0:T(1,128)}, u32[]{:S(2)}) copy-start(s32[1,128,1]{1,2,0:T(1,128)} %param.19) | copy-start | bytes 1540
  14.6 3.7 %copy-start.6 = (s32[8]{0:T(128)S(1)}, s32[8]{0:T(128)}, u32[]{:S(2)}) copy-start(s32[8]{0:T(128)} %param.18) | copy-start | bytes 100
  14.6 5.0 %copy-start.7 = (s32[8]{0:T(128)S(1)}, s32[8]{0:T(128)}, u32[]{:S(2)}) copy-start(s32[8]{0:T(128)} %param.17) | copy-start | bytes 100
  17.4 39.5 %collective-permute-start.2 = (bf16[1536,256]{1,0:T(8,128)(2,1)}, bf16[1536,256]{1,0:T(8,128)(2,1)}, u32[]{:S(2)}, u32[]{:S(2)}) collective-permute-start(bf16[1536,256]{1,0:T(8,128)(2,1)} %fusion.11), channel_id=1, source_target_pairs={{0,32},{32,0},{1,33},{33,1},{2,34},{34,2},{3,35},{35,3},{4,36},{36... | collective-permute-start | bytes 2359304 | tf_op jit(solution)/shard_map/ppermute | solution.py:417
  21.6 3.4 %copy-start.4 = (bf16[1,128,768]{2,1,0:T(8,128)(2,1)S(1)}, bf16[1,128,768]{2,1,0:T(8,128)(2,1)}, u32[]{:S(2)}) copy-start(bf16[1,128,768]{2,1,0:T(8,128)(2,1)} %param.12) | copy-start | bytes 589828
  48.4 22.1 %all-to-all-start.1 = ((bf16[32,120,128]{2,1,0:T(8,128)(2,1)}), bf16[32,120,128]{2,1,0:T(8,128)(2,1)S(1)}, u32[]{:S(2)}, u32[]{:S(2)}) async-start(bf16[32,120,128]{2,1,0:T(8,128)(2,1)} %attention_grads.1), calls=%async_computation.1 | async-start | bytes 1966080 | tf_op jit(solution)/shard_map/all_to_all | solution.py:25
  56.9 13.6 %copy-start = (bf16[768,1152]{1,0:T(8,128)(2,1)S(1)}, bf16[768,1152]{1,0:T(8,128)(2,1)}, u32[]{:S(2)}) copy-start(bf16[768,1152]{1,0:T(8,128)(2,1)} %weight.3) | copy-start | bytes 5308420
  72.5 6.3 %collective-permute-start.3 = (bf16[768,128]{1,0:T(8,128)(2,1)}, bf16[768,128]{1,0:T(8,128)(2,1)S(1)}, u32[]{:S(2)}, u32[]{:S(2)}) collective-permute-start(bf16[768,128]{1,0:T(8,128)(2,1)} %get-tuple-element.42), channel_id=1, source_target_pairs={{0,32},{32,0},{1,33},{33,1},{2,34},{34,2},{3,35},{35,3},{4,36},{36... | collective-permute-start | bytes 589832 | tf_op jit(solution)/shard_map/ppermute | solution.py:430
  73.9 14.5 %all-to-all-start.2 = ((bf16[32,8,768]{2,1,0:T(8,128)(2,1)}), bf16[32,8,768]{2,1,0:T(8,128)(2,1)S(1)}, u32[]{:S(2)}, u32[]{:S(2)}) async-start(bf16[32,8,768]{2,1,0:T(8,128)(2,1)} %bitcast.40), calls=%async_computation.2 | async-start | bytes 786432 | tf_op jit(solution)/shard_map/all_to_all | solution.py:25
  80.1 1.4 copy-start.1
  81.4 1.1 copy-start.8
  88.4 2.5 %collective-permute-start.4 = (bf16[256,768]{1,0:T(8,128)(2,1)S(1)}, bf16[256,768]{1,0:T(8,128)(2,1)S(1)}, u32[]{:S(2)}, u32[]{:S(2)}) collective-permute-start(bf16[256,768]{1,0:T(8,128)(2,1)S(1)} %bitcast.33), channel_id=1, source_target_pairs={{0,32},{32,0},{1,33},{33,1},{2,34},{34,2},{3,35},{35,3},{4,36},{36... | collective-permute-start | bytes 1179656 | tf_op jit(solution)/shard_map/ppermute | solution.py:456
  96.2 53.7 %all-to-all-start.3 = ((bf16[64,24,1152]{2,1,0:T(8,128)(2,1)}), bf16[64,24,1152]{2,1,0:T(8,128)(2,1)}, u32[]{:S(2)}, u32[]{:S(2)}) async-start(bf16[64,24,1152]{2,1,0:T(8,128)(2,1)} %bitcast.36), calls=%async_computation.3 | async-start | bytes 7077888 | tf_op jit(solution)/shard_map/all_to_all | solution.py:25
  152.5 2.3 %collective-permute-start.5 = (f32[12,1152]{1,0:T(8,128)S(1)}, f32[12,1152]{1,0:T(8,128)S(1)}, u32[]{:S(2)}, u32[]{:S(2)}) collective-permute-start(f32[12,1152]{1,0:T(8,128)S(1)} %get-tuple-element.55), channel_id=1, source_target_pairs={{0,32},{32,0},{1,33},{33,1},{2,34},{34,2},{3,35},{35,3},{4,36},{36... | collective-permute-start | bytes 165896 | tf_op jit(solution)/shard_map/ppermute | solution.py:465

commit v4 on v3

--- a/solution.py
+++ b/solution.py
@@ -196,7 +196,7 @@
     )(saved, cot, weight)
 
 
-def token_kernel(core, got, cot_t, weight, selector, routed, own, send, grads, *, heads, hd, ny):
+def token_kernel(core, got, cot, weight, selector, routed, own, send, grads, *, heads, hd, ny):
     tok = got.shape[2]
     sub = tok // ny
     part = 2 * hd // ny
@@ -215,7 +215,7 @@
         grads[rows[2], :] = total[hd:, :]
         grads[rows[3], :] = both[hd:, :]
     embed_t = jnp.dot(weight[...], grads[: 3 * width, :], preferred_element_type=F32)
-    embed_t = (cot_t[...].astype(F32) + embed_t).astype(BF16)
+    embed_t = (cot[...].astype(F32).T + embed_t).astype(BF16)
     routed[...] = lax.dot_general(
         selector[...], embed_t, (((1,), (1,)), ((), ())), preferred_element_type=F32
     ).astype(BF16)
@@ -231,8 +231,8 @@
         send[...] = grads[: 2 * width, :]
 
 
-def token_grads(core, got, cot_t, weight, selector, heads, hd, ny):
-    d_slide, tok = cot_t.shape
+def token_grads(core, got, cot, weight, selector, heads, hd, ny):
+    tok, d_slide = cot.shape
     vmem = pl.BlockSpec(memory_space=pltpu.VMEM)
     return pl.pallas_call(
         partial(token_kernel, heads=heads, hd=hd, ny=ny),
@@ -248,7 +248,7 @@
             flops=2 * weight.size * tok, bytes_accessed=4_000_000, transcendentals=0
         ),
         name="token_grads",
-    )(core, near(got), near(cot_t), near(weight), near(selector))
+    )(core, near(got), cot, near(weight), near(selector))
 
 
 def final_kernel(core, mine, pair, weight_t, proj, embed, qkv, out, *, half):
@@ -388,10 +388,9 @@
     ).astype(BF16)
     core_of = core.astype(jnp.int32).reshape(1)
     outgoing = packed(qkv_saved[0], cot, out_weight, heads, n_y)
-    outgoing, hidden_rows, output_rows, cot_later = lax.optimization_barrier(
-        (outgoing, tile_hidden[0], tile_output[0], cot)
-    )
-    cot_t = cot_later.T
+    outgoing, hidden_rows, output_rows = lax.optimization_barrier(
+        (outgoing, tile_hidden[0], tile_output[0])
+    )
     mine = exchange(outgoing, SEQ)
 
     seg = seg_length[head].astype(F32)
@@ -420,12 +419,12 @@
     cot_pair = jnp.concatenate([cot, swap(cot)], axis=0)
     first_rows = picked_rows(one_hot_rows(owner * half + spot, d_slide, ~second), embed_pair)
     second_rows = picked_rows(one_hot_rows(owner * half + spot, d_slide, second), embed_pair)
-    back, first_rows, second_rows, cot_pair, cot_t, selector = lax.optimization_barrier(
-        (back, first_rows, second_rows, cot_pair, cot_t, selector)
+    back, first_rows, second_rows, cot_pair, selector = lax.optimization_barrier(
+        (back, first_rows, second_rows, cot_pair, selector)
     )
     tile_rows = jnp.concatenate([keep, other], axis=1)
     got, tile_rows = lax.optimization_barrier((exchange(back, SEQ), tile_rows))
-    routed, own, send = token_grads(core_of, got, cot_t, qkv_weight, selector, heads, hd, n_y)
+    routed, own, send = token_grads(core_of, got, cot, qkv_weight, selector, heads, hd, n_y)
     incoming = exchange(routed.reshape(n_seq, capacity, d_slide), SEQ).reshape(-1, d_slide)
     grads = jnp.concatenate([own, swap(send)], axis=1)
     grads = grads.reshape(2, width, 2 * tok)
@@ -451,8 +450,8 @@
         [flat[0], jnp.where(low, flat[1], cot_pair[:, :width]), cot_pair[:, width:]], axis=0
     )
     small = jnp.dot(left_side, right_side, preferred_element_type=F32).astype(BF16)
+
     incoming, small = lax.optimization_barrier((incoming, small))
-
     term = summed_terms(tile_rows, incoming, swap(incoming), small)
     term = term.reshape(holders, -1, term.shape[1])
     held = jnp.sum(exchange(term, ("zh",) + SEQ).astype(F32), axis=0)

time: 158 us -> 157 us (level)
    unnamed x21 -> x20, local copies, waits for them, and re-layouts: 6.01 us -> 4.79 us
where the time goes in v4:
time: 157 us; the launch traced here: 155 us
  waiting for transfers between devices  56.8 us (36%)
  starting transfers between devices  30.6 us (19%)
  Pallas kernels  30 us (19%)
  matrix products  22.6 us (14%)
  local copies, waits for them, and re-layouts  6.25 us (4%)
  other arithmetic  6 us (4%)
  between operations  2.35 us (1%)
    all_to_all x4, waiting for transfers between devices, exchange(): return lax.all_to_all(x, axes, 0, 0, tiled=True)  54.5 us
    all_to_all x4, starting transfers between devices, exchange(): return lax.all_to_all(x, axes, 0, 0, tiled=True)  23.8 us
    pallas_call x1, Pallas kernels, attention_grads(): pl.pallas_call(partial(attention_kernel, hd=hd, tok=tok, nkb=nkb, ny=ny,...  17.6 us
    dot_general x4, matrix products, picked_rows(): jnp.einsum('rx,tx->rt', onehot, x, preferred_element_type=F32).astype(BF16)  11.5 us
    dot_general x1, matrix products, local(): jnp.einsum('se,fe->sf', tile_grad.astype(BF16), proj_weight, preferred_el...  5.97 us
    pallas_call x1, Pallas kernels, summed_terms(): pl.pallas_call(summed_kernel, grid=(count // block,), out_shape=jax.Shape...  5.24 us
    unnamed x20, local copies, waits for them, and re-layouts  4.79 us
  transfers between devices with their start and end apart: 10, of which 6 were waited for; matrix products, arithmetic and copies ran while one was open for 20% of the time, Pallas kernels for 13%

profile of v4, /device:TPU:1, one launch (start us, length us, event | category | flops | bytes accessed | tf_op | source)
XLA Modules:
  0.0 154.6 jit_solution(14301815310275605102)
XLA Ops:
  0.6 1.5 collective-permute-start
  2.2 2.6 %packed.1 = bf16[32,120,128]{2,1,0:T(8,128)(2,1)} custom-call(bf16[128,1152]{1,0:T(8,128)(2,1)} %bitcast.39, bf16[128,768]{1,0:T(8,128)(2,1)} %bitcast.32, bf16[384,768]{1,0:T(8,128)(2,1)} %weight.2), custom_call_target="tpu_custom_call" | custom-call | flops 75497472 | bytes 2000000 | tf_op jit(solution)/shard_map/packed/pallas_call | solution.py:187
  4.8 8.5 %all-to-all-start = ((bf16[32,120,128]{2,1,0:T(8,128)(2,1)}), bf16[32,120,128]{2,1,0:T(8,128)(2,1)S(1)}, u32[]{:S(2)}, u32[]{:S(2)}) async-start(bf16[32,120,128]{2,1,0:T(8,128)(2,1)} %packed.1), calls=%async_computation | async-start | bytes 1966080 | tf_op jit(solution)/shard_map/all_to_all | solution.py:25
  13.5 3.9 %fusion.11 = bf16[1536,256]{1,0:T(8,128)(2,1)} fusion(s32[1536]{0:T(1024)S(1)} %fusion.77, bf16[256,1536]{1,0:T(8,128)(2,1)S(1)} %bitcast.41, bf16[256,1536]{1,0:T(8,128)(2,1)} %bitcast.42, pred[]{:T(512)S(6)} %eq.143), kind=kOutput, calls=%fused_computation.14 | convolution fusion | flops 1211105280 | bytes 2365441 | tf_op jit(solution)/shard_map/rx,tx->rt/dot_general | solution.py:346
  20.9 2.3 %fusion.12 = bf16[1536,256]{1,0:T(8,128)(2,1)} fusion(s32[1536]{0:T(1024)S(1)} %fusion.74, pred[1536]{0:T(1024)(128)(4,1)S(1)} %fusion.69, bf16[128,768]{1,0:T(8,128)(2,1)S(1)} %collective-permute-done, bf16[128,768]{1,0:T(8,128)(2,1)S(1)} %bitcast.45), kind=kOutput, calls=%fused_computation.15 | convolution fusion | flops 607518720 | bytes 1187328 | tf_op jit(solution)/shard_map/rx,tx->rt/dot_general | solution.py:346
  23.2 2.3 %fusion.15 = bf16[1536,256]{1,0:T(8,128)(2,1)} fusion(s32[1536]{0:T(1024)S(1)} %fusion.74, pred[1536]{0:T(1024)(128)(4,1)S(1)} %fusion.89, bf16[128,768]{1,0:T(8,128)(2,1)S(1)} %collective-permute-done, bf16[128,768]{1,0:T(8,128)(2,1)S(1)} %bitcast.46), kind=kOutput, calls=%fused_computation.16 | convolution fusion | flops 607518720 | bytes 1187328 | tf_op jit(solution)/shard_map/rx,tx->rt/dot_general | solution.py:346
  25.5 4.1 %all-to-all-done.mine = bf16[32,120,128]{2,1,0:T(8,128)(2,1)S(1)} async-done(((bf16[32,120,128]{2,1,0:T(8,128)(2,1)}), bf16[32,120,128]{2,1,0:T(8,128)(2,1)S(1)}, u32[]{:S(2)}, u32[]{:S(2)}) %all-to-all-start) | async-done | bytes 983072 | tf_op jit(solution)/shard_map/all_to_all | solution.py:25
  29.6 17.6 %attention_grads.1 = bf16[32,120,128]{2,1,0:T(8,128)(2,1)} custom-call(f32[4]{0:T(128)} %pad_maximum_fusion.5.par, bf16[32,120,128]{2,1,0:T(8,128)(2,1)S(1)} %all-to-all-done.mine), custom_call_target="tpu_custom_call" | custom-call | flops 30000001024 | bytes 4000000 | tf_op jit(solution)/shard_map/attention_grads/pallas_call | solution.py:138
  47.2 3.9 %all-to-all-start.1 = ((bf16[32,120,128]{2,1,0:T(8,128)(2,1)}), bf16[32,120,128]{2,1,0:T(8,128)(2,1)S(1)}, u32[]{:S(2)}, u32[]{:S(2)}) async-start(bf16[32,120,128]{2,1,0:T(8,128)(2,1)} %attention_grads.1), calls=%async_computation.1 | async-start | bytes 1966080 | tf_op jit(solution)/shard_map/all_to_all | solution.py:25
  51.2 3.0 %fusion.10 = bf16[1536,256]{1,0:T(8,128)(2,1)S(1)} fusion(s32[1536]{0:T(1024)S(1)} %fusion.77, bf16[256,1536]{1,0:T(8,128)(2,1)} %bitcast.43, bf16[256,1536]{1,0:T(8,128)(2,1)} %bitcast.40, pred[]{:T(512)S(6)} %eq.143), kind=kOutput, calls=%fused_computation.13 | convolution fusion | flops 1211105280 | bytes 2365441 | tf_op jit(solution)/shard_map/rx,tx->rt/dot_general | solution.py:346
  54.2 2.5 %pad_maximum_fusion.rows = bf16[1536,512]{1,0:T(8,128)(2,1)} fusion(bf16[1536,256]{1,0:T(8,128)(2,1)} %collective-permute-done.2, bf16[1536,256]{1,0:T(8,128)(2,1)S(1)} %fusion.10), kind=kLoop, calls=%fused_computation.34 | loop fusion | flops 3145728 | bytes 3145728 | tf_op jit(solution)/shard_map/concatenate | solution.py:425
  56.7 9.8 %all-to-all-done.1.got = bf16[32,120,128]{2,1,0:T(8,128)(2,1)S(1)} async-done(((bf16[32,120,128]{2,1,0:T(8,128)(2,1)}), bf16[32,120,128]{2,1,0:T(8,128)(2,1)S(1)}, u32[]{:S(2)}, u32[]{:S(2)}) %all-to-all-start.1) | async-done | bytes 983072 | tf_op jit(solution)/shard_map/all_to_all | solution.py:25
  66.5 2.9 %token_grads.1 = (bf16[256,768]{1,0:T(8,128)(2,1)}, bf16[768,128]{1,0:T(8,128)(2,1)}, bf16[768,128]{1,0:T(8,128)(2,1)}) custom-call(s32[1]{0:T(128)} %bitcast.7.core, bf16[32,120,128]{2,1,0:T(8,128)(2,1)S(1)} %all-to-all-done.1.got, bf16[128,768]{1,0:T(8,128)(2,1)} %bitcast.33, bf16[768,1152]{1,0:T(8,128)(2,1)S(1)} %copy-done, ...), custom_call_target="tpu_custom_call" | custom-call | flops 226492416 | bytes 4000000 | tf_op jit(solution)/shard_map/token_grads/pallas_call | solution.py:237
  69.4 2.7 %collective-permute-start.3 = (bf16[768,128]{1,0:T(8,128)(2,1)}, bf16[768,128]{1,0:T(8,128)(2,1)S(1)}, u32[]{:S(2)}, u32[]{:S(2)}) collective-permute-start(bf16[768,128]{1,0:T(8,128)(2,1)} %get-tuple-element.38), channel_id=1, source_target_pairs={{0,32},{32,0},{1,33},{33,1},{2,34},{34,2},{3,35},{35,3},{4,36},{36... | collective-permute-start | bytes 589832 | tf_op jit(solution)/shard_map/ppermute | solution.py:429
  72.1 3.9 %all-to-all-start.2 = ((bf16[32,8,768]{2,1,0:T(8,128)(2,1)}), bf16[32,8,768]{2,1,0:T(8,128)(2,1)S(1)}, u32[]{:S(2)}, u32[]{:S(2)}) async-start(bf16[32,8,768]{2,1,0:T(8,128)(2,1)} %bitcast.38), calls=%async_computation.2 | async-start | bytes 786432 | tf_op jit(solution)/shard_map/all_to_all | solution.py:25
  76.0 1.0 constant_dynamic-update-slice_fusion.1
  77.3 1.3 fusion.18
  78.6 1.3 convolution_convert_fusion.4
  80.0 0.9 copy-done.8
  81.0 2.4 %convolution_convert_fusion.small = bf16[1536,384]{1,0:T(8,128)(2,1)} fusion(bf16[1536,256]{1,0:T(8,128)(2,1)S(1)} %fusion.18, bf16[1536,256]{1,0:T(8,128)(2,1)S(1)} %broadcast_select_fusion, bf16[1536,256]{1,0:T(8,128)(2,1)S(1)} %copy-done.8, bf16[256,384]{1,0:T(8,128)(2,1)S(1)} %get-tuple-element.50, bf16[256,384]{1,0:T(8,128)(2,1)S(1)} %get-tuple-element.49, ...), kind=kOutput, calls=%fused_computation.11 | convolution fusion | flops 915406848 | bytes 4128768 | tf_op jit(solution)/shard_map/dot_general | solution.py:452
  83.4 3.2 %all-to-all-done.2 = bf16[32,8,768]{2,1,0:T(8,128)(2,1)S(1)} async-done(((bf16[32,8,768]{2,1,0:T(8,128)(2,1)}), bf16[32,8,768]{2,1,0:T(8,128)(2,1)S(1)}, u32[]{:S(2)}, u32[]{:S(2)}) %all-to-all-start.2) | async-done | bytes 393248 | tf_op jit(solution)/shard_map/all_to_all | solution.py:25
  86.6 1.2 collective-permute-start.4
  87.8 1.3 collective-permute-done.4.swapped
  89.1 5.2 %summed_terms.1 = bf16[1536,1152]{1,0:T(8,128)(2,1)} custom-call(bf16[1536,512]{1,0:T(8,128)(2,1)} %pad_maximum_fusion.rows, bf16[256,768]{1,0:T(8,128)(2,1)S(1)} %bitcast.28, bf16[256,768]{1,0:T(8,128)(2,1)S(1)} %collective-permute-done.4.swapped, bf16[1536,384]{1,0:T(8,128)(2,1)} %convolution_convert_fusion.small), custom_call_target="tpu_custom_call" | custom-call | flops 1207959552 | bytes 8000000 | tf_op jit(solution)/shard_map/summed_terms/pallas_call | solution.py:318
  94.4 7.5 %all-to-all-start.3 = ((bf16[64,24,1152]{2,1,0:T(8,128)(2,1)}), bf16[64,24,1152]{2,1,0:T(8,128)(2,1)}, u32[]{:S(2)}, u32[]{:S(2)}) async-start(bf16[64,24,1152]{2,1,0:T(8,128)(2,1)} %bitcast.30), calls=%async_computation.3 | async-start | bytes 7077888 | tf_op jit(solution)/shard_map/all_to_all | solution.py:25
  101.8 2.8 %copy.21 = bf16[1536,768]{0,1:T(8,128)(2,1)S(1)} copy(bf16[1536,768]{1,0:T(8,128)(2,1)} %param.22) | data formatting | bytes 4718592 | tf_op args[10]
  104.7 6.0 %fusion.19 = bf16[1,256,1536]{2,1,0:T(8,128)(2,1)} fusion(bf16[1536,1536]{1,0:T(8,128)(2,1)} %param.23, bf16[256,768]{1,0:T(8,128)(2,1)S(1)} %bitcast.29, bf16[1536,768]{1,0:T(8,128)(2,1)} %param.22), kind=kOutput, calls=%fused_computation.21 | convolution fusion | flops 1812725760 | bytes 8257536 | tf_op jit(solution)/shard_map/se,fe->sf/dot_general | solution.py:459
  110.7 37.4 %all-to-all-done.3 = bf16[64,24,1152]{2,1,0:T(8,128)(2,1)} async-done(((bf16[64,24,1152]{2,1,0:T(8,128)(2,1)}), bf16[64,24,1152]{2,1,0:T(8,128)(2,1)}, u32[]{:S(2)}, u32[]{:S(2)}) %all-to-all-start.3) | async-done | bytes 3538976 | tf_op jit(solution)/shard_map/all_to_all | solution.py:25
  148.1 2.5 %convert_reduce_fusion = f32[24,1152]{1,0:T(8,128)S(1)} fusion(bf16[64,24,1152]{2,1,0:T(8,128)(2,1)} %all-to-all-done.3), kind=kLoop, calls=%fused_computation.3 | loop fusion | flops 3511296 | bytes 3649536 | tf_op jit(solution)/shard_map/reduce_sum | solution.py:457
  150.6 1.4 collective-permute-start.5
  152.0 0.9 collective-permute-done.5.pair
  152.9 1.7 %final_outputs.1 = (f32[12,1536]{1,0:T(8,128)}, f32[12,768]{1,0:T(8,128)}, f32[6,1152]{1,0:T(8,128)}, f32[3,768]{1,0:T(4,128)}) custom-call(s32[1]{0:T(128)} %bitcast.7.core, f32[12,1152]{1,0:T(8,128)S(1)} %get-tuple-element.52.mine, f32[12,1152]{1,0:T(8,128)S(1)} %collective-permute-done.5.pair, bf16[768,1536]{1,0:T(8,128)(2,1)S(1)} %bitcast.26), custom_call_target="tpu_custom_call" | custom-call | flops 84934656 | bytes 3000000 | tf_op jit(solution)/shard_map/final_outputs/pallas_call | solution.py:283
  (43 shorter events, 2.7 us)
Async XLA Ops:
  0.6 12.8 %copy-start.3 = (bf16[1,256,1536]{2,1,0:T(8,128)(2,1)S(1)}, bf16[1,256,1536]{2,1,0:T(8,128)(2,1)}, u32[]{:S(2)}) copy-start(bf16[1,256,1536]{2,1,0:T(8,128)(2,1)} %param.20) | copy-start | bytes 2359300
  0.6 20.3 %collective-permute-start = (bf16[128,768]{1,0:T(8,128)(2,1)}, bf16[128,768]{1,0:T(8,128)(2,1)S(1)}, u32[]{:S(2)}, u32[]{:S(2)}) collective-permute-start(bf16[128,768]{1,0:T(8,128)(2,1)} %bitcast.44), channel_id=1, source_target_pairs={{0,32},{32,0},{1,33},{33,1},{2,34},{34,2},{3,35},{35,3},{4,36},{36... | collective-permute-start | bytes 589832 | tf_op jit(solution)/shard_map/ppermute | solution.py:418
  2.1 18.8 %collective-permute-start.1 = (bf16[128,768]{1,0:T(8,128)(2,1)}, bf16[128,768]{1,0:T(8,128)(2,1)S(1)}, u32[]{:S(2)}, u32[]{:S(2)}) collective-permute-start(bf16[128,768]{1,0:T(8,128)(2,1)} %bitcast.31), channel_id=1, source_target_pairs={{0,32},{32,0},{1,33},{33,1},{2,34},{34,2},{3,35},{35,3},{4,36},{36... | collective-permute-start | bytes 589832 | tf_op jit(solution)/shard_map/ppermute | solution.py:419
  4.8 24.8 %all-to-all-start = ((bf16[32,120,128]{2,1,0:T(8,128)(2,1)}), bf16[32,120,128]{2,1,0:T(8,128)(2,1)S(1)}, u32[]{:S(2)}, u32[]{:S(2)}) async-start(bf16[32,120,128]{2,1,0:T(8,128)(2,1)} %packed.1), calls=%async_computation | async-start | bytes 1966080 | tf_op jit(solution)/shard_map/all_to_all | solution.py:25
  13.4 4.0 %copy-start.5 = (s32[1,128,1]{1,2,0:T(1,128)S(1)}, s32[1,128,1]{1,2,0:T(1,128)}, u32[]{:S(2)}) copy-start(s32[1,128,1]{1,2,0:T(1,128)} %param.19) | copy-start | bytes 1540
  13.4 4.2 %copy-start.6 = (s32[8]{0:T(128)S(1)}, s32[8]{0:T(128)}, u32[]{:S(2)}) copy-start(s32[8]{0:T(128)} %param.18) | copy-start | bytes 100
  13.4 5.5 %copy-start.7 = (s32[8]{0:T(128)S(1)}, s32[8]{0:T(128)}, u32[]{:S(2)}) copy-start(s32[8]{0:T(128)} %param.17) | copy-start | bytes 100
  13.4 7.4 %copy-start.1 = (bf16[1,128,768]{2,1,0:T(8,128)(2,1)S(1)}, bf16[1,128,768]{2,1,0:T(8,128)(2,1)}, u32[]{:S(2)}) copy-start(bf16[1,128,768]{2,1,0:T(8,128)(2,1)} %param.14) | copy-start | bytes 589828
  13.5 7.5 %copy-start.4 = (bf16[1,128,768]{2,1,0:T(8,128)(2,1)S(1)}, bf16[1,128,768]{2,1,0:T(8,128)(2,1)}, u32[]{:S(2)}) copy-start(bf16[1,128,768]{2,1,0:T(8,128)(2,1)} %param.12) | copy-start | bytes 589828
  17.4 36.8 %collective-permute-start.2 = (bf16[1536,256]{1,0:T(8,128)(2,1)}, bf16[1536,256]{1,0:T(8,128)(2,1)}, u32[]{:S(2)}, u32[]{:S(2)}) collective-permute-start(bf16[1536,256]{1,0:T(8,128)(2,1)} %fusion.11), channel_id=1, source_target_pairs={{0,32},{32,0},{1,33},{33,1},{2,34},{34,2},{3,35},{35,3},{4,36},{36... | collective-permute-start | bytes 2359304 | tf_op jit(solution)/shard_map/ppermute | solution.py:416
  47.2 19.3 %all-to-all-start.1 = ((bf16[32,120,128]{2,1,0:T(8,128)(2,1)}), bf16[32,120,128]{2,1,0:T(8,128)(2,1)S(1)}, u32[]{:S(2)}, u32[]{:S(2)}) async-start(bf16[32,120,128]{2,1,0:T(8,128)(2,1)} %attention_grads.1), calls=%async_computation.1 | async-start | bytes 1966080 | tf_op jit(solution)/shard_map/all_to_all | solution.py:25
  54.2 12.3 %copy-start = (bf16[768,1152]{1,0:T(8,128)(2,1)S(1)}, bf16[768,1152]{1,0:T(8,128)(2,1)}, u32[]{:S(2)}) copy-start(bf16[768,1152]{1,0:T(8,128)(2,1)} %weight.3) | copy-start | bytes 5308420
  69.4 7.6 %collective-permute-start.3 = (bf16[768,128]{1,0:T(8,128)(2,1)}, bf16[768,128]{1,0:T(8,128)(2,1)S(1)}, u32[]{:S(2)}, u32[]{:S(2)}) collective-permute-start(bf16[768,128]{1,0:T(8,128)(2,1)} %get-tuple-element.38), channel_id=1, source_target_pairs={{0,32},{32,0},{1,33},{33,1},{2,34},{34,2},{3,35},{35,3},{4,36},{36... | collective-permute-start | bytes 589832 | tf_op jit(solution)/shard_map/ppermute | solution.py:429
  72.1 14.5 %all-to-all-start.2 = ((bf16[32,8,768]{2,1,0:T(8,128)(2,1)}), bf16[32,8,768]{2,1,0:T(8,128)(2,1)S(1)}, u32[]{:S(2)}, u32[]{:S(2)}) async-start(bf16[32,8,768]{2,1,0:T(8,128)(2,1)} %bitcast.38), calls=%async_computation.2 | async-start | bytes 786432 | tf_op jit(solution)/shard_map/all_to_all | solution.py:25
  78.5 1.4 copy-start.2
  79.8 1.1 copy-start.8
  86.6 2.5 %collective-permute-start.4 = (bf16[256,768]{1,0:T(8,128)(2,1)S(1)}, bf16[256,768]{1,0:T(8,128)(2,1)S(1)}, u32[]{:S(2)}, u32[]{:S(2)}) collective-permute-start(bf16[256,768]{1,0:T(8,128)(2,1)S(1)} %bitcast.27), channel_id=1, source_target_pairs={{0,32},{32,0},{1,33},{33,1},{2,34},{34,2},{3,35},{35,3},{4,36},{36... | collective-permute-start | bytes 1179656 | tf_op jit(solution)/shard_map/ppermute | solution.py:455
  94.4 53.7 %all-to-all-start.3 = ((bf16[64,24,1152]{2,1,0:T(8,128)(2,1)}), bf16[64,24,1152]{2,1,0:T(8,128)(2,1)}, u32[]{:S(2)}, u32[]{:S(2)}) async-start(bf16[64,24,1152]{2,1,0:T(8,128)(2,1)} %bitcast.30), calls=%async_computation.3 | async-start | bytes 7077888 | tf_op jit(solution)/shard_map/all_to_all | solution.py:25
  150.6 2.3 %collective-permute-start.5 = (f32[12,1152]{1,0:T(8,128)S(1)}, f32[12,1152]{1,0:T(8,128)S(1)}, u32[]{:S(2)}, u32[]{:S(2)}) collective-permute-start(f32[12,1152]{1,0:T(8,128)S(1)} %get-tuple-element.51), channel_id=1, source_target_pairs={{0,32},{32,0},{1,33},{33,1},{2,34},{34,2},{3,35},{35,3},{4,36},{36... | collective-permute-start | bytes 165896 | tf_op jit(solution)/shard_map/ppermute | solution.py:464
